TPU v7x, 8 devices: a whole 2x2x1 slice. The times are simulated.
8 devices in a mesh: dp: 1 (over z), sp: 8 (over y, x, core).
Axes of the slice: x: 2, y: 2, z: 1, core: 2. Of those that a mesh axis runs over, the one named last changes fastest.
Arguments:
- latent: bfloat16 [16, 64, 64, 4], P('dp', 'sp')
- time_emb: bfloat16 [16, 1280], P('dp')
- w_in: bfloat16 [3, 3, 4, 320], replicated
- b_in: bfloat16 [320], replicated
- gn1_scale: bfloat16 [2, 320], replicated
- gn1_shift: bfloat16 [2, 320], replicated
- conv1_w: bfloat16 [2, 3, 3, 320, 320], replicated
- conv1_b: bfloat16 [2, 320], replicated
- temb_w: bfloat16 [2, 1280, 320], replicated
- temb_b: bfloat16 [2, 320], replicated
- gn2_scale: bfloat16 [2, 320], replicated
- gn2_shift: bfloat16 [2, 320], replicated
- conv2_w: bfloat16 [2, 3, 3, 320, 320], replicated
- conv2_b: bfloat16 [2, 320], replicated
- down_w: bfloat16 [3, 3, 320, 320], replicated
- down_b: bfloat16 [320], replicated
Outputs:
- output 1: bfloat16 [16, 64, 64, 320], P('dp', 'sp')
- output 2: bfloat16 [16, 64, 64, 320], P('dp', 'sp')
- output 3: bfloat16 [16, 64, 64, 320], P('dp', 'sp')
- output 4: bfloat16 [16, 32, 32, 320], P('dp', 'sp')
All inputs are finite; a program needn't handle non-finite values.
Results may differ from a plain program's by a relative error of at most 0.0134219.
Values are sent between devices in bfloat16 or wider.
A program may use at most 1 GiB of HBM per device.

v0:
```python
import jax
import jax.numpy as jnp
from jax import lax
from jax.sharding import PartitionSpec as P

GN_GROUPS = 32
GN_EPS = 1e-5
DIM_NUMS = ("NHWC", "HWIO", "NHWC")


def conv_valid_rows(inputs, kernel, bias_c, stride):
    out_f32 = lax.conv_general_dilated(inputs, kernel, (stride, stride), ((0, 0), (1, 1)), dimension_numbers=DIM_NUMS, preferred_element_type=jnp.float32)
    return (out_f32 + bias_c.astype(jnp.float32)).astype(jnp.bfloat16)


def group_sums(values):
    batch_n, rows_n, cols_n, chan_n = values.shape
    grouped = values.reshape(batch_n, rows_n * cols_n, GN_GROUPS, chan_n // GN_GROUPS)
    return jnp.stack([grouped.sum(axis=(1, 3)), jnp.square(grouped).sum(axis=(1, 3))], axis=-1)


def norm_silu(values, sums_all, elem_count, gain_c, shift_c):
    group_ch = values.shape[-1] // GN_GROUPS
    grp_mean = sums_all[..., 0] / elem_count
    grp_var = sums_all[..., 1] / elem_count - grp_mean * grp_mean
    inv_std = lax.rsqrt(grp_var + GN_EPS)
    scale_bc = jnp.repeat(inv_std, group_ch, axis=1) * gain_c.astype(jnp.float32)
    offset_bc = shift_c.astype(jnp.float32) - jnp.repeat(grp_mean, group_ch, axis=1) * scale_bc
    return jax.nn.silu(values * scale_bc[:, None, None, :] + offset_bc[:, None, None, :]).astype(jnp.bfloat16)


def solution(mesh):
    sp_size = mesh.shape["sp"]
    to_next = [(device, device + 1) for device in range(sp_size - 1)]
    to_prev = [(device + 1, device) for device in range(sp_size - 1)]

    def row_from_above(band_block):
        return lax.ppermute(band_block[:, -1:], "sp", to_next)

    def row_from_below(band_block):
        return lax.ppermute(band_block[:, :1], "sp", to_prev)

    def conv_band(band_block, kernel, bias_c):
        padded = jnp.concatenate([row_from_above(band_block), band_block, row_from_below(band_block)], axis=1)
        return conv_valid_rows(padded, kernel, bias_c, 1)

    def band_program(latent, time_emb, w_in, b_in, gn1_scale, gn1_shift, conv1_w, conv1_b, temb_w, temb_b, gn2_scale, gn2_shift, conv2_w, conv2_b, down_w, down_b):
        elem_count = latent.shape[1] * sp_size * latent.shape[2] * (w_in.shape[-1] // GN_GROUPS)
        emb_act = jax.nn.silu(time_emb.astype(jnp.float32)).astype(jnp.bfloat16)
        hidden = conv_band(latent, w_in, b_in)
        outputs = [hidden]
        for layer_idx in range(conv1_w.shape[0]):
            hidden_f32 = hidden.astype(jnp.float32)
            sums_all = lax.psum(group_sums(hidden_f32), "sp")
            normed = norm_silu(hidden_f32, sums_all, elem_count, gn1_scale[layer_idx], gn1_shift[layer_idx])
            branch = conv_band(normed, conv1_w[layer_idx], conv1_b[layer_idx])
            emb_proj = jnp.dot(emb_act, temb_w[layer_idx], preferred_element_type=jnp.float32) + temb_b[layer_idx].astype(jnp.float32)
            mixed_in = branch.astype(jnp.float32) + emb_proj[:, None, None, :]
            sums_all = lax.psum(group_sums(mixed_in), "sp")
            normed = norm_silu(mixed_in, sums_all, elem_count, gn2_scale[layer_idx], gn2_shift[layer_idx])
            branch = conv_band(normed, conv2_w[layer_idx], conv2_b[layer_idx])
            hidden = (hidden_f32 + branch.astype(jnp.float32)).astype(jnp.bfloat16)
            outputs.append(hidden)
        padded = jnp.concatenate([row_from_above(hidden), hidden], axis=1)
        outputs.append(conv_valid_rows(padded, down_w, down_b, 2))
        return tuple(outputs)

    band_spec = P("dp", "sp", None, None)
    return jax.shard_map(band_program, mesh=mesh, in_specs=(band_spec, P("dp", None)) + (P(),) * 14, out_specs=(band_spec,) * 4, check_vma=False)
```

profile of v0, /device:TPU:0, one launch (start us, length us, event | category | flops | bytes accessed | tf_op | source)
XLA Modules:
  0.0 378.7 jit_solution(11296770459878460687)
XLA Ops:
  0.6 1.5 copy.42
  2.2 2.8 collective-permute-start
  5.0 1.3 collective-permute-start.1
  6.3 0.8 convert_reduce_fusion.7
  7.1 0.7 convert_element_type.126
  7.8 2.5 collective-permute-done.1
  10.2 6.7 %convert_reduce_fusion.1 = (f32[16,320]{1,0:T(8,128)S(1)}, f32[16,320]{1,0:T(8,128)S(1)}, bf16[16,8,64,320]{3,0,2,1:T(8,128)(2,1)}) fusion(f32[320]{0:T(512)S(1)} %convert_element_type.126, bf16[3,3,4,320]{3,2,1,0:T(4,128)(2,1)} %param.18, bf16[16,1,64,4]{0,3,2,1:T(4,128)(2,1)S(1)} %collective-permute-done.1, bf16[16,8,64,4]{0,3,2,1:T(4,128)(2,1)S(1)} %copy.42, ...), kind=kOutput, calls=%fused_computation.7 | convolution fusion | flops 202741760 | bytes 5390080 | tf_op jit(solution)/shard_map/conv_general_dilated | solution.py:12
  17.0 0.3 reduce_sum.96
  17.2 0.3 reduce_sum.99
  17.8 25.7 %psum.28 = f32[16,32,2]{1,0,2:T(8,128)S(1)} all-reduce(f32[16,32,2]{1,0,2:T(8,128)S(1)} %pad_maximum_fusion), channel_id=1, replica_groups=mesh['dp'=1,'sp'=8] {'sp'}, use_global_device_ids=true, to_apply=%region_4.5 | all-reduce | flops 1024 | bytes 8192 | tf_op jit(solution)/shard_map/psum | solution.py:54
  43.7 0.2 reshape.300
  44.0 0.2 reshape.301
  44.2 5.8 %fusion.7 = bf16[16,8,64,320]{3,0,2,1:T(8,128)(2,1)S(1)} fusion(bf16[16,8,64,320]{3,0,2,1:T(8,128)(2,1)} %get-tuple-element.60, f32[16,320]{1,0:T(8,128)S(1)} %get-tuple-element.48, f32[16,320]{1,0:T(8,128)S(1)} %get-tuple-element.49), kind=kLoop, calls=%fused_computation.15 | loop fusion | flops 20971520 | bytes 10526720 | tf_op jit(solution)/shard_map/convert_element_type | solution.py:29
  50.0 0.2 fusion.110
  50.2 1.3 collective-permute-start.2
  51.5 1.8 collective-permute-start.3
  53.4 0.3 convolution_add_fusion.1
  53.8 4.4 %collective-permute-done.3 = bf16[16,1,64,320]{3,0,2,1:T(8,128)(2,1)S(1)} collective-permute-done((bf16[16,1,64,320]{3,0,2,1:T(8,128)(2,1)S(1)}, bf16[16,1,64,320]{3,0,2,1:T(8,128)(2,1)S(1)}, u32[]{:S(2)}, u32[]{:S(2)}) %collective-permute-start.3) | collective-permute-done | bytes 655392 | tf_op jit(solution)/shard_map/ppermute | solution.py:41
  58.2 30.6 %fusion.19 = (f32[16,320]{1,0:T(8,128)S(1)}, f32[16,320]{1,0:T(8,128)S(1)}, bf16[16,8,64,320]{3,0,2,1:T(8,128)(2,1)}) fusion(f32[16,320]{1,0:T(8,128)S(1)} %convolution_add_fusion.1, f32[320]{0:T(512)S(1)} %get-tuple-element.39, bf16[2,3,3,320,320]{4,3,2,1,0:T(8,128)(2,1)} %param.22, bf16[16,1,64,320]{3,0,2,1:T(8,128)(2,1)S(1)} %collective-permute-done.3, ...), kind=kOutput, calls=%fused_computation.36 | convolution fusion | flops 14980208640 | bytes 14071040 | tf_op jit(solution)/shard_map/conv_general_dilated | solution.py:12
  88.8 0.3 reduce_sum.105
  89.1 0.1 reduce_sum.106
  89.2 0.3 reduce_sum.111
  89.5 0.1 reduce_sum.112
  89.6 36.0 %psum.29 = f32[16,32,2]{1,0,2:T(8,128)S(1)} all-reduce(f32[16,32,2]{1,0,2:T(8,128)S(1)} %pad_maximum_fusion.1), channel_id=1, replica_groups=mesh['dp'=1,'sp'=8] {'sp'}, use_global_device_ids=true, to_apply=%region_9.10 | all-reduce | flops 1024 | bytes 8192 | tf_op jit(solution)/shard_map/psum | solution.py:59
  125.7 0.2 reshape.302
  126.0 0.2 reshape.303
  126.2 5.9 %multiply_convert_fusion.1 = bf16[16,8,64,320]{3,0,2,1:T(8,128)(2,1)S(1)} fusion(bf16[16,8,64,320]{3,0,2,1:T(8,128)(2,1)} %get-tuple-element.61, f32[16,320]{1,0:T(8,128)S(1)} %get-tuple-element.46, f32[16,320]{1,0:T(8,128)S(1)} %get-tuple-element.47, f32[16,320]{1,0:T(8,128)S(1)} %convolution_add_fusion.1), kind=kLoop, calls=%fused_computation.33 | loop fusion | flops 23592960 | bytes 10547200 | tf_op jit(solution)/shard_map/convert_element_type | solution.py:29
  132.2 0.2 fusion.109
  132.3 1.3 collective-permute-start.4
  133.7 1.5 collective-permute-start.5
  135.2 0.3 collective-permute-done.4
  135.5 4.8 %collective-permute-done.5 = bf16[16,1,64,320]{3,0,2,1:T(8,128)(2,1)S(1)} collective-permute-done((bf16[16,1,64,320]{3,0,2,1:T(8,128)(2,1)S(1)}, bf16[16,1,64,320]{3,0,2,1:T(8,128)(2,1)S(1)}, u32[]{:S(2)}, u32[]{:S(2)}) %collective-permute-start.5) | collective-permute-done | bytes 655392 | tf_op jit(solution)/shard_map/ppermute | solution.py:41
  140.3 31.9 %convert_reduce_fusion = (f32[16,320]{1,0:T(8,128)S(1)}, f32[16,320]{1,0:T(8,128)S(1)}, bf16[16,8,64,320]{3,0,2,1:T(8,128)(2,1)}) fusion(f32[320]{0:T(512)S(1)} %get-tuple-element.41, bf16[2,3,3,320,320]{4,3,2,1,0:T(8,128)(2,1)} %param.28, bf16[16,1,64,320]{3,0,2,1:T(8,128)(2,1)S(1)} %collective-permute-done.5, ...), kind=kOutput, calls=%fused_computation.3 | convolution fusion | flops 14988072960 | bytes 20342016 | tf_op jit(solution)/shard_map/conv_general_dilated | solution.py:12
  172.2 0.3 reduce_sum.114
  172.5 0.1 reduce_sum.115
  172.6 0.3 reduce_sum.144
  173.1 37.3 %psum.30 = f32[16,32,2]{1,0,2:T(8,128)S(1)} all-reduce(f32[16,32,2]{1,0,2:T(8,128)S(1)} %pad_maximum_fusion.2), channel_id=1, replica_groups=mesh['dp'=1,'sp'=8] {'sp'}, use_global_device_ids=true, to_apply=%region_14.15 | all-reduce | flops 1024 | bytes 8192 | tf_op jit(solution)/shard_map/psum | solution.py:54
  210.5 0.2 reshape.304
  210.8 0.2 reshape.305
  211.0 5.8 %fusion.16 = bf16[16,8,64,320]{3,0,2,1:T(8,128)(2,1)S(1)} fusion(bf16[16,8,64,320]{3,0,2,1:T(8,128)(2,1)} %get-tuple-element.62, f32[16,320]{1,0:T(8,128)S(1)} %get-tuple-element.44, f32[16,320]{1,0:T(8,128)S(1)} %get-tuple-element.45), kind=kLoop, calls=%fused_computation.24 | loop fusion | flops 20971520 | bytes 10526720 | tf_op jit(solution)/shard_map/convert_element_type | solution.py:29
  216.8 0.2 fusion.108
  217.0 1.3 collective-permute-start.6
  218.3 1.5 collective-permute-start.7
  219.9 0.3 convolution_add_fusion
  220.2 4.8 %collective-permute-done.7 = bf16[16,1,64,320]{3,0,2,1:T(8,128)(2,1)S(1)} collective-permute-done((bf16[16,1,64,320]{3,0,2,1:T(8,128)(2,1)S(1)}, bf16[16,1,64,320]{3,0,2,1:T(8,128)(2,1)S(1)}, u32[]{:S(2)}, u32[]{:S(2)}) %collective-permute-start.7) | collective-permute-done | bytes 655392 | tf_op jit(solution)/shard_map/ppermute | solution.py:41
  225.0 30.6 %fusion.18 = (f32[16,320]{1,0:T(8,128)S(1)}, f32[16,320]{1,0:T(8,128)S(1)}, bf16[16,8,64,320]{3,0,2,1:T(8,128)(2,1)}) fusion(f32[16,320]{1,0:T(8,128)S(1)} %convolution_add_fusion, f32[320]{0:T(512)S(1)} %get-tuple-element.38, bf16[2,3,3,320,320]{4,3,2,1,0:T(8,128)(2,1)} %param.22, bf16[16,1,64,320]{3,0,2,1:T(8,128)(2,1)S(1)} %collective-permute-done.7, ...), kind=kOutput, calls=%fused_computation.30 | convolution fusion | flops 14980208640 | bytes 14071040 | tf_op jit(solution)/shard_map/conv_general_dilated | solution.py:12
  255.6 0.3 reduce_sum.147
  256.0 0.3 reduce_sum.150
  256.5 36.0 %psum.31 = f32[16,32,2]{1,0,2:T(8,128)S(1)} all-reduce(f32[16,32,2]{1,0,2:T(8,128)S(1)} %pad_maximum_fusion.3), channel_id=1, replica_groups=mesh['dp'=1,'sp'=8] {'sp'}, use_global_device_ids=true, to_apply=%region_19.20 | all-reduce | flops 1024 | bytes 8192 | tf_op jit(solution)/shard_map/psum | solution.py:59
  292.6 0.2 reshape.306
  292.9 0.2 reshape.307
  293.1 6.7 %multiply_convert_fusion = bf16[16,8,64,320]{3,0,2,1:T(8,128)(2,1)S(1)} fusion(bf16[16,8,64,320]{3,0,2,1:T(8,128)(2,1)} %get-tuple-element.63, f32[16,320]{1,0:T(8,128)S(1)} %get-tuple-element.42, f32[16,320]{1,0:T(8,128)S(1)} %get-tuple-element.43, f32[16,320]{1,0:T(8,128)S(1)} %convolution_add_fusion), kind=kLoop, calls=%fused_computation.27 | loop fusion | flops 23592960 | bytes 10547200 | tf_op jit(solution)/shard_map/convert_element_type | solution.py:29
  299.8 0.2 fusion.107
  299.9 1.3 collective-permute-start.8
  301.3 1.7 collective-permute-start.9
  303.1 4.8 %collective-permute-done.9 = bf16[16,1,64,320]{3,0,2,1:T(8,128)(2,1)S(1)} collective-permute-done((bf16[16,1,64,320]{3,0,2,1:T(8,128)(2,1)S(1)}, bf16[16,1,64,320]{3,0,2,1:T(8,128)(2,1)S(1)}, u32[]{:S(2)}, u32[]{:S(2)}) %collective-permute-start.9) | collective-permute-done | bytes 655392 | tf_op jit(solution)/shard_map/ppermute | solution.py:41
  307.9 29.3 %fusion.17 = bf16[16,8,64,320]{3,0,2,1:T(8,128)(2,1)S(1)} fusion(bf16[16,8,64,320]{3,0,2,1:T(8,128)(2,1)} %get-tuple-element.62, f32[320]{0:T(512)S(1)} %get-tuple-element.40, bf16[16,1,64,320]{3,0,2,1:T(8,128)(2,1)S(1)} %collective-permute-done.9, bf16[16,8,64,320]{3,0,2,1:T(8,128)(2,1)S(1)} %multiply_convert_fusion, ...), kind=kOutput, calls=%fused_computation.25 | convolution fusion | flops 14977597440 | bytes 20301056 | tf_op jit(solution)/shard_map/conv_general_dilated | solution.py:12
  337.2 2.7 copy-done.1
  339.9 17.4 %collective-permute-start.10 = (bf16[16,1,64,320]{3,0,2,1:T(8,128)(2,1)S(1)}, bf16[16,1,64,320]{3,0,2,1:T(8,128)(2,1)S(1)}, u32[]{:S(2)}, u32[]{:S(2)}) collective-permute-start(bf16[16,1,64,320]{3,0,2,1:T(8,128)(2,1)S(1)} %slice.174), channel_id=1, source_target_pairs={{0,1},{1,2},{2,3},{3,4},{4,5},{5,6},{6,7}} | collective-permute-start | bytes 1966088 | tf_op jit(solution)/shard_map/ppermute | solution.py:38
  357.4 4.3 %copy.45 = bf16[16,8,64,320]{3,2,1,0:T(8,128)(2,1)} copy(bf16[16,8,64,320]{3,0,2,1:T(8,128)(2,1)S(1)} %bitcast.83) | data formatting | bytes 10485760
  361.7 4.3 %copy.46 = bf16[16,8,64,320]{3,2,1,0:T(8,128)(2,1)} copy(bf16[16,8,64,320]{3,0,2,1:T(8,128)(2,1)S(1)} %bitcast.85) | data formatting | bytes 10485760
  366.0 4.3 %copy.47 = bf16[16,8,64,320]{3,2,1,0:T(8,128)(2,1)} copy(bf16[16,8,64,320]{3,0,2,1:T(8,128)(2,1)S(1)} %copy-done.2) | data formatting | bytes 10485760
  370.3 6.7 %add_convert_fusion.5 = bf16[16,4,32,320]{3,0,2,1:T(8,128)(2,1)S(1)} fusion(bf16[3,3,320,320]{3,2,1,0:T(8,128)(2,1)S(1)} %copy-done, bf16[16,8,64,320]{3,0,2,1:T(8,128)(2,1)S(1)} %copy-done.2, bf16[16,1,64,320]{3,0,2,1:T(8,128)(2,1)S(1)} %collective-permute-done.10, f32[320]{0:T(512)S(1)} %convert_element_type.154), kind=kOutput, calls=%fused_computation.67 | convolution fusion | flops 3748659200 | bytes 9053440 | tf_op jit(solution)/shard_map/conv_general_dilated | solution.py:12
  377.0 1.5 copy.48
  (74 shorter events, 2.3 us)
Async XLA Ops:
  0.6 369.7 %copy-start = (bf16[3,3,320,320]{3,2,1,0:T(8,128)(2,1)S(1)}, bf16[3,3,320,320]{3,2,1,0:T(8,128)(2,1)}, u32[]{:S(2)}) copy-start(bf16[3,3,320,320]{3,2,1,0:T(8,128)(2,1)} %param.30) | copy-start | bytes 5529604
  2.2 5.6 %collective-permute-start = (bf16[16,1,64,4]{0,3,2,1:T(4,128)(2,1)S(1)}, bf16[16,1,64,4]{0,3,2,1:T(4,128)(2,1)S(1)}, u32[]{:S(2)}, u32[]{:S(2)}) collective-permute-start(bf16[16,1,64,4]{0,3,2,1:T(4,128)(2,1)S(1)} %get-tuple-element.58), channel_id=1, source_target_pairs={{0,1},{1,2},{2,3},{3,4},{4,5},{5,6},{6,7}} | collective-permute-start | bytes 24584 | tf_op jit(solution)/shard_map/ppermute | solution.py:38
  5.0 5.2 %collective-permute-start.1 = (bf16[16,1,64,4]{0,3,2,1:T(4,128)(2,1)S(1)}, bf16[16,1,64,4]{0,3,2,1:T(4,128)(2,1)S(1)}, u32[]{:S(2)}, u32[]{:S(2)}) collective-permute-start(bf16[16,1,64,4]{0,3,2,1:T(4,128)(2,1)S(1)} %get-tuple-element.59), channel_id=1, source_target_pairs={{1,0},{2,1},{3,2},{4,3},{5,4},{6,5},{7,6}} | collective-permute-start | bytes 24584 | tf_op jit(solution)/shard_map/ppermute | solution.py:41
  44.1 9.1 %copy-start.3 = (bf16[2,320]{1,0:T(2,128)(2,1)S(1)}, bf16[2,320]{1,0:T(2,128)(2,1)}, u32[]{:S(2)}) copy-start(bf16[2,320]{1,0:T(2,128)(2,1)} %param.25) | copy-start | bytes 3844
  44.2 9.2 %copy-start.4 = (bf16[2,320]{1,0:T(2,128)(2,1)S(1)}, bf16[2,320]{1,0:T(2,128)(2,1)}, u32[]{:S(2)}) copy-start(bf16[2,320]{1,0:T(2,128)(2,1)} %param.23) | copy-start | bytes 3844
  44.2 9.2 %copy-start.5 = (bf16[2,320]{1,0:T(2,128)(2,1)S(1)}, bf16[2,320]{1,0:T(2,128)(2,1)}, u32[]{:S(2)}) copy-start(bf16[2,320]{1,0:T(2,128)(2,1)} %param.27) | copy-start | bytes 3844
  44.2 9.2 %copy-start.6 = (bf16[2,320]{1,0:T(2,128)(2,1)S(1)}, bf16[2,320]{1,0:T(2,128)(2,1)}, u32[]{:S(2)}) copy-start(bf16[2,320]{1,0:T(2,128)(2,1)} %param.26) | copy-start | bytes 3844
  44.2 9.2 %copy-start.9 = (bf16[2,1280,320]{1,2,0:T(8,128)(2,1)S(1)}, bf16[2,1280,320]{1,2,0:T(8,128)(2,1)}, u32[]{:S(2)}) copy-start(bf16[2,1280,320]{1,2,0:T(8,128)(2,1)} %param.24) | copy-start | bytes 4915204
  44.2 9.2 %copy-start.11 = (bf16[16,1280]{1,0:T(8,128)(2,1)S(1)}, bf16[16,1280]{1,0:T(8,128)(2,1)}, u32[]{:S(2)}) copy-start(bf16[16,1280]{1,0:T(8,128)(2,1)} %param.17) | copy-start | bytes 122884
  50.2 3.6 collective-permute-start.2
  51.5 6.6 %collective-permute-start.3 = (bf16[16,1,64,320]{3,0,2,1:T(8,128)(2,1)S(1)}, bf16[16,1,64,320]{3,0,2,1:T(8,128)(2,1)S(1)}, u32[]{:S(2)}, u32[]{:S(2)}) collective-permute-start(bf16[16,1,64,320]{3,0,2,1:T(8,128)(2,1)S(1)} %get-tuple-element.57), channel_id=1, source_target_pairs={{1,0},{2,1},{3,2},{4,3},{5,4},{6,5},{7,6}} | collective-permute-start | bytes 1966088 | tf_op jit(solution)/shard_map/ppermute | solution.py:41
  126.2 8.9 %copy-start.7 = (bf16[2,320]{1,0:T(2,128)(2,1)S(1)}, bf16[2,320]{1,0:T(2,128)(2,1)}, u32[]{:S(2)}) copy-start(bf16[2,320]{1,0:T(2,128)(2,1)} %param.29) | copy-start | bytes 3844
  132.3 3.2 collective-permute-start.4
  133.7 6.6 %collective-permute-start.5 = (bf16[16,1,64,320]{3,0,2,1:T(8,128)(2,1)S(1)}, bf16[16,1,64,320]{3,0,2,1:T(8,128)(2,1)S(1)}, u32[]{:S(2)}, u32[]{:S(2)}) collective-permute-start(bf16[16,1,64,320]{3,0,2,1:T(8,128)(2,1)S(1)} %get-tuple-element.55), channel_id=1, source_target_pairs={{1,0},{2,1},{3,2},{4,3},{5,4},{6,5},{7,6}} | collective-permute-start | bytes 1966088 | tf_op jit(solution)/shard_map/ppermute | solution.py:41
  211.0 8.8 %copy-start.10 = (bf16[2,1280,320]{1,2,0:T(8,128)(2,1)S(1)}, bf16[2,1280,320]{1,2,0:T(8,128)(2,1)}, u32[]{:S(2)}) copy-start(bf16[2,1280,320]{1,2,0:T(8,128)(2,1)} %param.24) | copy-start | bytes 4915204
  217.0 3.2 collective-permute-start.6
  218.3 6.6 %collective-permute-start.7 = (bf16[16,1,64,320]{3,0,2,1:T(8,128)(2,1)S(1)}, bf16[16,1,64,320]{3,0,2,1:T(8,128)(2,1)S(1)}, u32[]{:S(2)}, u32[]{:S(2)}) collective-permute-start(bf16[16,1,64,320]{3,0,2,1:T(8,128)(2,1)S(1)} %get-tuple-element.53), channel_id=1, source_target_pairs={{1,0},{2,1},{3,2},{4,3},{5,4},{6,5},{7,6}} | collective-permute-start | bytes 1966088 | tf_op jit(solution)/shard_map/ppermute | solution.py:41
  293.1 64.3 %slice-start = ((s8[6291456]{0:T(1024)(128)(4,1)}), s8[4194304]{0:T(1024)(128)(4,1)S(1)}, s32[]{:S(2)}) async-start(s8[6291456]{0:T(1024)(128)(4,1)} %bitcast.82), calls=%async_computation | async-start | bytes 8388608
  293.1 68.6 %slice-start.2 = ((s8[6291456]{0:T(1024)(128)(4,1)}), s8[4194304]{0:T(1024)(128)(4,1)S(1)}, s32[]{:S(2)}) async-start(s8[6291456]{0:T(1024)(128)(4,1)} %bitcast.84), calls=%async_computation.2 | async-start | bytes 8388608
  299.9 3.2 collective-permute-start.8
  301.3 6.6 %collective-permute-start.9 = (bf16[16,1,64,320]{3,0,2,1:T(8,128)(2,1)S(1)}, bf16[16,1,64,320]{3,0,2,1:T(8,128)(2,1)S(1)}, u32[]{:S(2)}, u32[]{:S(2)}) collective-permute-start(bf16[16,1,64,320]{3,0,2,1:T(8,128)(2,1)S(1)} %get-tuple-element.51), channel_id=1, source_target_pairs={{1,0},{2,1},{3,2},{4,3},{5,4},{6,5},{7,6}} | collective-permute-start | bytes 1966088 | tf_op jit(solution)/shard_map/ppermute | solution.py:41
  307.9 49.5 %copy-start.8 = (bf16[320]{0:T(512)(128)(2,1)S(1)}, bf16[320]{0:T(512)(128)(2,1)}, u32[]{:S(2)}) copy-start(bf16[320]{0:T(512)(128)(2,1)} %param.31) | copy-start | bytes 1924
  307.9 49.5 %slice-start.1 = ((s8[6291456]{0:T(1024)(128)(4,1)}), s8[2097152]{0:T(1024)(128)(4,1)S(1)}, s32[]{:S(2)}) async-start(s8[6291456]{0:T(1024)(128)(4,1)} %bitcast.82), calls=%async_computation.1 | async-start | bytes 4194304
  307.9 53.8 %slice-start.3 = ((s8[6291456]{0:T(1024)(128)(4,1)}), s8[2097152]{0:T(1024)(128)(4,1)S(1)}, s32[]{:S(2)}) async-start(s8[6291456]{0:T(1024)(128)(4,1)} %bitcast.84), calls=%async_computation.3 | async-start | bytes 4194304
  337.2 2.7 copy-start.1
  339.9 30.4 %collective-permute-start.10 = (bf16[16,1,64,320]{3,0,2,1:T(8,128)(2,1)S(1)}, bf16[16,1,64,320]{3,0,2,1:T(8,128)(2,1)S(1)}, u32[]{:S(2)}, u32[]{:S(2)}) collective-permute-start(bf16[16,1,64,320]{3,0,2,1:T(8,128)(2,1)S(1)} %slice.174), channel_id=1, source_target_pairs={{0,1},{1,2},{2,3},{3,4},{4,5},{5,6},{6,7}} | collective-permute-start | bytes 1966088 | tf_op jit(solution)/shard_map/ppermute | solution.py:38
  361.7 4.3 %copy-start.2 = (bf16[16,8,64,320]{3,0,2,1:T(8,128)(2,1)S(1)}, bf16[16,8,64,320]{3,0,2,1:T(8,128)(2,1)}, u32[]{:S(2)}) copy-start(bf16[16,8,64,320]{3,0,2,1:T(8,128)(2,1)} %copy-done.1) | copy-start | bytes 15728644
where the time goes:
time: 384 us; the launch traced here: 379 us
  matrix products  136 us (35%)
  blocking collectives  135 us (35%)
  starting transfers between devices  33.3 us (9%)
  other arithmetic  27 us (7%)
  local copies, waits for them, and re-layouts  23.8 us (6%)
  waiting for transfers between devices  21.7 us (6%)
    conv_general_dilated x6, matrix products, conv_valid_rows(): lax.conv_general_dilated(inputs, kernel, (stride, stride), ((0, 0), (1, 1...  136 us
    psum x2, blocking collectives, band_program(): sums_all = lax.psum(group_sums(mixed_in), 'sp')  71.9 us
    psum x2, blocking collectives, band_program(): sums_all = lax.psum(group_sums(hidden_f32), 'sp')  63 us
    ppermute x6, starting transfers between devices, row_from_above(): return lax.ppermute(band_block[:, -1:], 'sp', to_next)  25.6 us
    convert_element_type x4, other arithmetic, norm_silu(): jax.nn.silu(values * scale_bc[:, None, None, :] + offset_bc[:, None, None...  24.2 us
    ppermute x5, waiting for transfers between devices, row_from_below(): return lax.ppermute(band_block[:, :1], 'sp', to_prev)  21.2 us
    unnamed x37, local copies, waits for them, and re-layouts  18.6 us
    ppermute x5, starting transfers between devices, row_from_below(): return lax.ppermute(band_block[:, :1], 'sp', to_prev)  7.71 us
  transfers between devices with their start and end apart: 11, of which 7 were waited for; matrix products, arithmetic and copies ran while one was open for 4% of the time, Pallas kernels for 0%

commit v1 on v0

v1 whole, which is shorter than its diff:
```python
import functools

import jax
import jax.numpy as jnp
from jax import lax
from jax.experimental import pallas as pl
from jax.experimental.pallas import tpu as pltpu
from jax.sharding import PartitionSpec as P

F32, BF = jnp.float32, jnp.bfloat16
GN_GROUPS, GN_EPS = 32, 1e-5
NS, ROWS, ROW, LANE, MAIN = 16, 8, 64, 128, 256
NP = ROWS * ROW
CH = 320
CP = CH + ROW
KP = 4 * MAIN
REST = 3 * MAIN
SPARE = 3 * CH
OFF = 8
MESH = pl.DeviceIdType.MESH


def span(i, n=ROW, base=0):
    return slice(base + i * n, base + (i + 1) * n)


def low_half():
    return lax.broadcasted_iota(jnp.int32, (ROW, LANE), 1) < ROW


def widen(p):
    return jnp.concatenate([p, p[..., MAIN:]], -1)


def keep_if(flag, x):
    return jnp.where(jnp.full(x.shape, flag, jnp.int32) > 0, x, 0.0)


def store_rest(L, o, r0, r1, r2):
    low = low_half()
    L[span(o), REST:REST + LANE] = jnp.where(low, r0, r1).astype(BF)
    L[span(o), REST + LANE:] = jnp.where(low, r2, 1.0).astype(BF)


def prep_gen(x_of_row, nrows, a, b, L):
    ha, hb = a * 0.5, b * 0.5
    rest = []
    for r in range(nrows + 2):
        x, flag = x_of_row(r)
        h = x.astype(F32) * ha + hb
        n = h + h * jnp.tanh(h)
        if flag is not None:
            n = keep_if(flag, n)
        main = n[:, :MAIN].astype(BF)
        rest.append(n[:, MAIN:])
        for dy in range(3):
            if 0 <= r - dy < nrows:
                L[span(r - dy), span(dy, MAIN)] = main
        if r >= 2:
            store_rest(L, r - 2, *rest[r - 2:])
        yield


def conv_row(Y, o, zero):
    sub = lax.broadcasted_iota(jnp.int32, (8, LANE), 0)
    top, bot = sub == 0, sub == 7

    def here(k):
        return Y[k, span(o, base=OFF), :]

    def left(k):
        v = Y[k, pl.ds(zero + (OFF - 1 + o * ROW), ROW), :]
        return jnp.concatenate([jnp.where(top, 0.0, v[:8]), v[8:]], 0)

    def right(k):
        v = Y[k, pl.ds(zero + (OFF + 1 + o * ROW), ROW), :]
        return jnp.concatenate([v[:-8], jnp.where(bot, 0.0, v[-8:])], 0)

    out = [left(k) + here(k + 2) + right(k + 4) for k in range(2)]
    mix = jnp.where(low_half(), left(6), here(6))
    return out + [mix + pltpu.roll(mix, ROW, 1) + right(7)]


def dot_chunk(L, W, Y, rows, n):
    r = jnp.dot(L[rows, :], W[:, span(n, 2 * MAIN)], preferred_element_type=F32)
    for k in range(4):
        Y[4 * n + k, OFF + rows.start:OFF + rows.stop, :] = r[:, span(k, LANE)]


def weave(chunks, gens):
    live = list(gens)
    steps = 0
    for c in chunks:
        c()
        steps += 1
        for _ in range(6):
            for g in list(live):
                if next(g, StopIteration) is StopIteration:
                    live.remove(g)
    for g in live:
        for _ in g:
            pass


def lane_left(x, k):
    return pltpu.roll(x, CP - k, 1)


def affine(tots, gain, shift, embs, sp):
    z = [jnp.zeros((4 - len(tots), CP), F32)] * (len(tots) < 4)
    s = jnp.concatenate([jnp.concatenate([t[k:k + 1] for k in range(3)], 1) for t in tots] + z, 0)
    q = jnp.concatenate([jnp.concatenate([t[k + 3:k + 4] for k in range(3)], 1) for t in tots] + z, 0)
    e = jnp.concatenate(list(embs) + z, 0)
    npos = float(sp * NP)
    x = jnp.concatenate([s + npos * e, q + e * (2.0 * s + npos * e)], 0)
    lane = lax.broadcasted_iota(jnp.int32, (8, CP), 1)
    w2 = x + lane_left(x, 1)
    w4 = w2 + lane_left(w2, 2)
    w8 = w4 + lane_left(w4, 4)
    w10 = w8 + lane_left(w2, 8)
    size = CH // GN_GROUPS
    y = jnp.where((lane % size == 0) & (lane < CH), w10, 0.0)
    r2 = y + pltpu.roll(y, 1, 1)
    r4 = r2 + pltpu.roll(r2, 2, 1)
    r8 = r4 + pltpu.roll(r4, 4, 1)
    r = r8 + pltpu.roll(r2, 8, 1)
    r = jnp.where(lane >= CH, pltpu.roll(r, ROW, 1), r) * (1.0 / (npos * size))
    mean, msq = r[:4], r[4:]
    a = gain * lax.rsqrt(msq - mean * mean + GN_EPS)
    return a, shift + a * (e - mean)


def stats_tile(acc, acq):
    parts = [x.sum(0, keepdims=True) for x in acc + acq]
    return jnp.concatenate(parts + [jnp.zeros((2, LANE), F32)], 0)


def add_stats(acc, acq, new):
    for k, x in enumerate(new):
        v = x.astype(F32).reshape(8, 8, LANE)
        acc[k] = acc[k] + v.sum(0)
        acq[k] = acq[k] + (v * v).sum(0)


def no_stats():
    return [jnp.zeros((8, LANE), F32) for _ in range(3)]


def weight_copies(src, W, WR, sem_main, sem_rest):
    for dy in range(3):
        for dx in range(3):
            cols = span(dx, MAIN)
            pltpu.make_async_copy(src.at[dy, dx, :MAIN, :MAIN], W.at[span(dy, MAIN), cols], sem_main).start()
            pltpu.make_async_copy(src.at[dy, dx, MAIN:, :MAIN], W.at[span(dy, base=REST), cols], sem_main).start()
            pltpu.make_async_copy(src.at[dy, dx, :, MAIN:], WR.at[dy * 3 + dx], sem_rest).start()


def weight_finish(W, WR, bias, sem_main, sem_rest):
    main = W.at[:SPARE, :REST]
    pltpu.make_async_copy(main, main, sem_main).wait()
    pltpu.make_async_copy(WR, WR, sem_rest).wait()
    for dy in range(3):
        for part, rows in ((slice(0, MAIN), span(dy, MAIN)), (slice(MAIN, CH), span(dy, base=REST))):
            w0, w1, w2 = (WR[dy * 3 + dx, part, :] for dx in range(3))
            W[rows, REST:REST + LANE] = jnp.concatenate([w0, w1], 1)
            W[rows, REST + LANE:] = jnp.concatenate([w2, w2], 1)
    b = widen(bias.astype(F32))
    gap = jnp.zeros((1, MAIN), F32)
    rest = jnp.where(low_half()[:1], 0.0, b[:, MAIN:])
    row = jnp.concatenate([gap, b[:, :MAIN], gap, rest, gap[:, :LANE]], 1)
    first = lax.broadcasted_iota(jnp.int32, (ROW, KP), 0) == 0
    W[SPARE:, :] = jnp.where(first, row, 0.0).astype(BF)


def mega(sp, q, qx, edges, win, temb, tb, g1, s1, g2, s2, b1, b2, tw, w1, w2, hand, hand0, halo, abo,
         H, U, H2, HS, W, WR, TW, L0, L1, Y0, Y1, ST, RS, AB, EMB, GAIN, HT, HB, HX, LQ,
         wm_sem, wr_sem, tw_sem, q_send, q_recv, st_send, st_recv, up_send, dn_send, x_send, ht_recv, hb_recv, hx_recv, out_sem, fin_sem):
    me, dp = lax.axis_index("sp"), lax.axis_index("dp")
    has_up, has_dn = (me > 0).astype(jnp.int32), (me < sp - 1).astype(jnp.int32)
    held = (H, U, H2, U)

    get_tw = pltpu.make_async_copy(tw, TW, tw_sem)
    get_tw.start()
    for j, src in enumerate((w1.at[0], w2.at[0], w1.at[1])):
        weight_copies(src, W.at[j], WR.at[j], wm_sem.at[j], wr_sem.at[j])

    barrier = pltpu.get_barrier_semaphore()
    for k in range(1, sp):
        pl.semaphore_signal(barrier, inc=1, device_id=(dp, lax.rem(me + k, sp)), device_id_type=MESH)
    pl.semaphore_wait(barrier, sp - 1)

    def remote(src, dst, ssem, rsem, dev):
        return pltpu.make_async_remote_copy(src_ref=src, dst_ref=dst, send_sem=ssem, recv_sem=rsem, device_id=(dp, dev), device_id_type=MESH)

    q_dn = remote(edges.at[0], LQ.at[0], q_send.at[0], q_recv.at[0], me + 1)
    q_up = remote(edges.at[1], LQ.at[1], q_send.at[1], q_recv.at[1], me - 1)

    def if_up(f):
        pl.when(me > 0)(f)

    def if_dn(f):
        pl.when(me < sp - 1)(f)

    if_dn(q_dn.start)
    if_up(q_up.start)

    def up_copy(slot, s):
        return remote(held[slot].at[s, :ROW], HB.at[slot, s], up_send.at[slot, s], hb_recv.at[slot, s], me - 1)

    def dn_copy(slot, s):
        return remote(held[slot].at[s, NP - ROW:], HT.at[slot, s], dn_send.at[slot, s], ht_recv.at[slot, s], me + 1)

    def dx_copy(s):
        return remote(U.at[s, NP - 2 * ROW:NP - ROW], HX.at[s], x_send.at[s], hx_recv.at[s], me + 1)

    def out_copy(slot, s):
        src, dst = ((HS, hand0), None, (H2, hand.at[0]), (U, hand.at[1]))[slot]
        return pltpu.make_async_copy(src.at[s], dst.at[s], out_sem.at[slot, s])

    def send(slot, s):
        for k in range(1, sp):
            remote(ST.at[slot, s], RS.at[slot, s, k - 1], st_send.at[slot, s], st_recv.at[slot, s], lax.rem(me + k, sp)).start()
        if slot != 1:
            out_copy(slot, s).start()
        if_up(lambda: up_copy(slot, s).start())

        def down():
            dn_copy(slot, s).start()
            if slot == 3:
                dx_copy(s).start()
        if_dn(down)

    def wait_stats(slot, s):
        pltpu.make_async_copy(RS.at[slot, s], RS.at[slot, s], st_recv.at[slot, s]).wait()

    def wait_halo(slot, s):
        if_up(lambda: remote(H.at[s, :ROW], HT.at[slot, s], dn_send.at[slot, s], ht_recv.at[slot, s], me).wait_recv())
        if_dn(lambda: remote(H.at[s, :ROW], HB.at[slot, s], up_send.at[slot, s], hb_recv.at[slot, s], me).wait_recv())

    def wait_sent(slot, s):
        if_up(lambda: up_copy(slot, s).wait_send())
        if_dn(lambda: dn_copy(slot, s).wait_send())

    for k, (ref, l) in enumerate(((g1, 0), (g2, 0), (g1, 1), (g2, 1), (s1, 0), (s2, 0), (s1, 1), (s2, 1))):
        GAIN[k:k + 1, :] = widen(ref[l:l + 1, :].astype(F32))
    get_tw.wait()
    x = temb[...].astype(F32)
    act = (x * jax.nn.sigmoid(x)).astype(BF)
    for l in range(2):
        pr = lax.dot_general(act, TW[l], (((1,), (1,)), ((), ())), preferred_element_type=F32)
        EMB[2 * l] = jnp.zeros((NS, CP), F32)
        EMB[2 * l + 1] = widen(pr + tb[l:l + 1, :].astype(F32))

    if_up(q_dn.wait_recv)
    if_dn(q_up.wait_recv)
    lane16 = lax.broadcasted_iota(jnp.int32, (NS, LANE), 1) < ROW

    def first(s):
        e0 = qx[s, :, :LANE].astype(F32)
        e1 = qx[s, :, NP:].astype(F32)
        e0 = jnp.where(lane16, keep_if(has_up, LQ[0, s].astype(F32)), e0).astype(BF)
        e1 = jnp.where(lane16, e1, keep_if(has_dn, LQ[1, s].astype(F32))).astype(BF)
        lhs = jnp.concatenate([
            jnp.concatenate([e0, qx[s, :, LANE:NP]], 1), q[s],
            jnp.concatenate([qx[s, :, LANE:NP], e1], 1)], 0)
        r = lax.dot_general(lhs, win[...], (((0,), (0,)), ((), ())), preferred_element_type=F32)
        acc, acq = no_stats(), no_stats()
        for o in range(ROWS):
            x = r[span(o), :].astype(BF)
            H[s, span(o), :] = x
            HS[s, span(o), :] = x[:, :CH]
            add_stats(acc, acq, [x[:, span(k, LANE)] for k in range(3)])
        ST[0, s] = stats_tile(acc, acq)

    def first_pair(i, carry):
        @pl.when(i > 0)
        def _():
            send(0, 2 * i - 2)
            send(0, 2 * i - 1)
        first(2 * i)
        first(2 * i + 1)
        return carry

    lax.fori_loop(0, NS // 2, first_pair, 0)
    for j in range(3):
        weight_finish(W.at[j], WR.at[j], (b1, b2)[j % 2][j // 2:j // 2 + 1, :], wm_sem.at[j], wr_sem.at[j])
    send(0, NS - 2)
    send(0, NS - 1)

    def total(slot, s):
        t = ST[slot, s]
        for k in range(sp - 1):
            t = t + RS[slot, s, k]
        return t

    def scales(slot, ss):
        a, b = affine([total(slot, s) for s in ss], GAIN[pl.ds(slot, 1)], GAIN[pl.ds(slot + 4, 1)],
                      [EMB[slot, pl.ds(s, 1)] for s in ss], sp)

        def store(dst):
            for k, s in enumerate(ss):
                dst[0, pl.ds(s, 1)] = a[k:k + 1]
                dst[1, pl.ds(s, 1)] = b[k:k + 1]
        return store

    def prep_of(slot, s, L, a, b):
        def row(r):
            if r == 0:
                return HT[slot, s], has_up
            if r == ROWS + 1:
                return HB[slot, s], has_dn
            return held[slot][s, span(r - 1), :], None
        return prep_gen(row, ROWS, a, b, L)

    def epi_gen(j, s, Y, zero):
        acc, acq = no_stats(), no_stats()
        for o in range(ROWS):
            new = [x.astype(BF) for x in conv_row(Y, o, zero)]
            for k in range(3):
                if j == 1:
                    new[k] = (new[k].astype(F32) + H[s, span(o), span(k, LANE)].astype(F32)).astype(BF)
                held[j + 1][s, span(o), span(k, LANE)] = new[k]
            add_stats(acc, acq, new)
            yield
        ST[j + 1, s] = stats_tile(acc, acq)

    def coeffs(s):
        return AB[0, pl.ds(s, 1)], AB[1, pl.ds(s, 1)]

    def half(j, t, Lc, Ln, Yc, Yp, zero):
        nxt = jnp.minimum(t + 1, NS - 1)
        chunks = [functools.partial(dot_chunk, Lc, W.at[j], Yc, slice(0, NP), n) for n in range(2)]
        weave(chunks, (prep_of(j, nxt, Ln, *coeffs(nxt)), epi_gen(j, lax.rem(t + NS - 1, NS), Yp, zero)))

    for s in range(4):
        wait_stats(0, s)
    scales(0, range(4))(AB)
    wait_halo(0, 0)
    for j in range(3):
        if j == 2:
            def sent(s, carry):
                wait_sent(1, s)
                return carry
            lax.fori_loop(0, NS, sent, 0)
        for _ in prep_of(j, 0, L0, *coeffs(0)):
            pass
        if j > 0:
            send(j, NS - 1)

        def body(i, carry, j=j):
            t = 2 * i
            zero = jnp.minimum(i, 0) * 8
            ns = [j * NS + t + k for k in (4, 5)]
            slot = ns[0] // NS
            ss = [lax.rem(n, NS) for n in ns]
            for s in ss:
                pl.when(slot < 3)(functools.partial(wait_stats, slot, s))
            for n in (j * NS + t + 1, j * NS + t + 2):
                wait_halo(n // NS, lax.rem(n, NS))

            @pl.when(i > 0)
            def _():
                send(j + 1, t - 2)

            @pl.when(i > 1)
            def _():
                send(j + 1, t - 3)
            store = scales(jnp.minimum(slot, 2), ss)
            half(j, t, L0, L1, Y0, Y1, zero)
            half(j, t + 1, L1, L0, Y1, Y0, zero)
            store(AB)
            return carry

        lax.fori_loop(0, NS // 2, body, 0)
        send(j + 1, NS - 3)
        send(j + 1, NS - 2)
        for _ in epi_gen(j, NS - 1, Y1, jnp.minimum(me, 0) * 8):
            pass

    send(3, NS - 1)

    def drain(s, carry):
        wait_stats(3, s)
        for slot in range(4):
            pltpu.make_async_copy(RS.at[slot, s], RS.at[slot, s], st_send.at[slot, s]).wait()
            if slot != 1:
                out_copy(slot, s).wait()
                wait_sent(slot, s)
        pl.when(s > 0)(lambda: wait_halo(3, s))
        if_up(lambda: dx_copy(s).wait_recv())
        if_dn(lambda: dx_copy(s).wait_send())
        return carry

    lax.fori_loop(0, NS, drain, 0)
    if_dn(q_dn.wait_send)
    if_up(q_up.wait_send)
    fins = [pltpu.make_async_copy(r, halo.at[k], fin_sem.at[k]) for k, r in enumerate((HT.at[2], HT.at[3], HX, HB.at[3]))]
    for f in fins:
        f.start()
    for k in range(4):
        scales(3, range(4 * k, 4 * k + 4))(abo)
    for f in fins:
        f.wait()


def tail(hand, hand0, halo, ab, b2, bd, w2, dw, h0o, h1o, h2o, do,
         H, U, HA, P0, X2, W, WR, L0, L1, Y0, Y1, O1, O2, OD, DS, in_sem, ha_sem, p_sem, wm_sem, wr_sem, o_sem, od_sem):
    me, sp = lax.axis_index("sp"), lax.axis_size("sp")
    has_up, has_dn = (me > 0).astype(jnp.int32), (me < sp - 1).astype(jnp.int32)
    get_halo = pltpu.make_async_copy(halo, HA, ha_sem)
    get_halo.start()

    def get(k, s):
        return pltpu.make_async_copy(hand.at[k, s], (H, U)[k].at[s], in_sem.at[k, s])

    def take0(s):
        return pltpu.make_async_copy(hand0.at[s], P0.at[s], p_sem.at[s])

    for k in (1, 0):
        get(k, 0).start()
    for j, src in enumerate((w2.at[1], dw)):
        weight_copies(src, W.at[j], WR.at[j], wm_sem.at[j], wr_sem.at[j])

    def fetch(s, carry):
        for k in (1, 0):
            get(k, s).start()
        return carry

    lax.fori_loop(1, NS, fetch, 0)

    def fetch0(s, carry):
        take0(s).start()
        return carry

    lax.fori_loop(0, NS, fetch0, 0)

    def ready(s):
        for k in (1, 0):
            get(k, s).wait()

    def prep_of(s, L):
        def row(r):
            if r < 2:
                return HA[2 - r, s], has_up
            if r == ROWS + 2:
                return HA[3, s], has_dn
            return U[s, span(r - 2), :], None
        return prep_gen(row, ROWS + 1, ab[0, pl.ds(s, 1)], ab[1, pl.ds(s, 1)], L)

    def epi_gen(s, Y, zero):
        for o in range(ROWS + 1):
            t = conv_row(Y, o, zero)
            for k in range(3):
                cols = span(k, LANE)
                old = HA[0, s, :, cols] if o == 0 else H[s, span(o - 1), cols]
                new = old.astype(F32) + t[k].astype(BF).astype(F32)
                new = (keep_if(has_up, new) if o == 0 else new).astype(BF)
                X2[s, span(o), cols] = new
                if o > 0:
                    n = min(LANE, CH - k * LANE)
                    cols = slice(k * LANE, k * LANE + n)
                    O1[s, span(o - 1), cols] = old[:, :n]
                    O2[s, span(o - 1), cols] = new[:, :n]
            yield

    def put(k, s):
        src, dst = ((P0, h0o), (O1, h1o), (O2, h2o))[k]
        return pltpu.make_async_copy(src.at[s], dst.at[s], o_sem.at[k, s])

    def half(t, Lc, Ln, Yc, Yp, zero):
        chunks = [functools.partial(dot_chunk, Lc, W.at[0], Yc, slice(0, NP + ROW), n) for n in range(2)]
        weave(chunks, (prep_of(jnp.minimum(t + 1, NS - 1), Ln), epi_gen(lax.rem(t + NS - 1, NS), Yp, zero)))

    get_halo.wait()
    ready(0)
    for _ in prep_of(0, L0):
        pass
    for j in range(2):
        weight_finish(W.at[j], WR.at[j], (b2[1:2, :], bd[...])[j], wm_sem.at[j], wr_sem.at[j])

    def body(i, carry):
        t = 2 * i
        zero = jnp.minimum(i, 0) * 8
        ready(t + 1)
        pl.when(t + 2 < NS)(lambda: ready(t + 2))
        for n in (t, t + 1):
            take0(n).wait()
            put(0, n).start()
        for n in (t - 3, t - 2):
            @pl.when(n >= 0)
            def _(n=n):
                put(1, n).start()
                put(2, n).start()
        half(t, L0, L1, Y0, Y1, zero)
        half(t + 1, L1, L0, Y1, Y0, zero)
        return carry

    lax.fori_loop(0, NS // 2, body, 0)
    still = jnp.minimum(me, 0) * 8
    for _ in epi_gen(NS - 1, Y1, still):
        pass
    for s in range(NS - 3, NS):
        put(1, s).start()
        put(2, s).start()

    def dprep(s, L):
        for o in range(4):
            xs = [X2[s, span(2 * o + dy), :] for dy in range(3)]
            for dy in range(3):
                L[span(o), span(dy, MAIN)] = xs[dy][:, :MAIN]
            store_rest(L, o, *(x[:, MAIN:].astype(F32) for x in xs))

    def depi(s, Y, zero):
        for o in range(4):
            d = conv_row(Y, o, zero)
            for k in range(3):
                DS[o, k] = d[k]
            parts = [DS[o, k, pl.ds(0, ROW // 2, stride=2), :] for k in range(3)]
            OD[s, span(o, ROW // 2), :] = jnp.concatenate(parts, 1)[:, :CH].astype(BF)

    def dhalf(t, Lc, Ln, Yc, Yp, zero):
        for n in range(2):
            dot_chunk(Lc, W.at[1], Yc, slice(0, NP // 2), n)
        dprep(jnp.minimum(t + 1, NS - 1), Ln)
        depi(lax.rem(t + NS - 1, NS), Yp, zero)

    dprep(0, L0)

    def dbody(i, carry):
        t = 2 * i
        zero = jnp.minimum(i, 0) * 8
        dhalf(t, L0, L1, Y0, Y1, zero)
        dhalf(t + 1, L1, L0, Y1, Y0, zero)
        return carry

    lax.fori_loop(0, NS // 2, dbody, 0)
    depi(NS - 1, Y1, still)
    dout = pltpu.make_async_copy(OD, do, od_sem)
    dout.start()

    def drain(s, carry):
        for k in range(3):
            put(k, s).wait()
        return carry

    lax.fori_loop(0, NS, drain, 0)
    dout.wait()


def solution(mesh):
    sp = mesh.shape["sp"]

    def program(latent, time_emb, w_in, b_in, gn1_scale, gn1_shift, conv1_w, conv1_b, temb_w, temb_b, gn2_scale, gn2_shift, conv2_w, conv2_b, down_w, down_b):
        none = (0, 0)
        lat = jnp.pad(latent.transpose(0, 3, 1, 2), (none, none, none, (1, 1)))
        q = jnp.stack([lat[..., d:d + ROW] for d in range(3)], 1).reshape(NS, 12, NP)
        q = jnp.pad(q, (none, (0, 4), none), constant_values=1)
        qx = jnp.pad(q, (none, none, (ROW, ROW)))
        edges = jnp.stack([jnp.pad(q[..., NP - ROW:], (none, none, (0, ROW))), jnp.pad(q[..., :ROW], (none, none, (ROW, 0)))])
        spare = jnp.zeros((3, 4, CH), BF).at[1, 0].set(b_in)
        win = widen(jnp.concatenate([w_in.reshape(3, 12, CH), spare], 1).reshape(3 * NS, CH))

        dma, vm = pltpu.SemaphoreType.DMA, pltpu.VMEM
        any_, vms = pl.BlockSpec(memory_space=pl.ANY), pl.BlockSpec(memory_space=pltpu.VMEM)
        params = functools.partial(pltpu.CompilerParams, vmem_limit_bytes=66_000_000)

        def big(n=NP, c=CP):
            return vm((NS, n, c), BF)

        def bufs(m):
            return [vm((m, KP), BF)] * 2 + [vm((8, m + 2 * OFF, LANE), F32)] * 2

        def out(*shape):
            return jax.ShapeDtypeStruct(shape, BF)

        hand, hand0, halo, ab = pl.pallas_call(
            functools.partial(mega, sp),
            out_shape=(out(2, NS, NP, CP), out(NS, NP, CH), out(4, NS, ROW, CP), jax.ShapeDtypeStruct((2, NS, CP), F32)),
            in_specs=[vms, vms, any_] + [vms] * 9 + [any_] * 3, out_specs=(any_, any_, any_, vms),
            scratch_shapes=[big(), big(), big(), big(NP, CH), vm((3, KP, KP), BF), vm((3, 9, CH, ROW), BF), vm((2, CH, temb_w.shape[1]), BF)] + bufs(NP)
            + [vm((4, NS, 8, LANE), F32), vm((4, NS, sp - 1, 8, LANE), F32), vm((2, NS, CP), F32), vm((4, NS, CP), F32), vm((8, CP), F32),
               vm((4, NS, ROW, CP), BF), vm((4, NS, ROW, CP), BF), big(ROW), vm((2, NS, NS, LANE), BF),
               dma((3,)), dma((3,)), dma, dma((2,)), dma((2,)), dma((4, NS)), dma((4, NS)), dma((4, NS)), dma((4, NS)), dma((NS,)),
               dma((4, NS)), dma((4, NS)), dma((NS,)), dma((4, NS)), dma((4,))],
            compiler_params=params(collective_id=0, has_side_effects=True), name="mega",
        )(q, qx, edges, win, time_emb, temb_b, gn1_scale, gn1_shift, gn2_scale, gn2_shift, conv1_b, conv2_b, temb_w.transpose(0, 2, 1), conv1_w, conv2_w)
        outs = pl.pallas_call(
            tail,
            out_shape=(out(NS, NP, CH),) * 3 + (out(NS, NP // 4, CH),),
            in_specs=[any_] * 3 + [vms] * 3 + [any_] * 2, out_specs=(any_,) * 4,
            scratch_shapes=[big(), big(), vm((4, NS, ROW, CP), BF), big(NP, CH), big(NP + ROW), vm((2, KP, KP), BF), vm((2, 9, CH, ROW), BF)] + bufs(NP + ROW)
            + [big(NP, CH), big(NP, CH), big(NP // 4, CH), vm((4, 3, ROW, LANE), F32),
               dma((2, NS)), dma, dma((NS,)), dma((2,)), dma((2,)), dma((3, NS)), dma],
            compiler_params=params(), name="tail",
        )(hand, hand0, halo, ab, conv2_b, down_b.reshape(1, CH), conv2_w, down_w)
        return tuple(o.reshape(NS, n, m, CH) for o, n, m in zip(outs, (ROWS,) * 3 + (ROWS // 2,), (ROW,) * 3 + (ROW // 2,)))

    band = P("dp", "sp", None, None)
    return jax.shard_map(program, mesh=mesh, in_specs=(band, P("dp", None)) + (P(),) * 14, out_specs=(band,) * 4, check_vma=False)
```

time: 384 us -> 172 us (0.45); the launches traced: 379 us -> 171 us
  Pallas kernels: 0 us -> 162 us
  matrix products: 136 us -> 0 us
  blocking collectives: 135 us -> 0 us
  starting transfers between devices: 33.3 us -> 0 us
  other arithmetic: 27 us -> 2.66 us
  waiting for transfers between devices: 21.7 us -> 0 us
  local copies, waits for them, and re-layouts: 23.8 us -> 5.38 us
    pallas_call x0 -> x2, Pallas kernels: none -> 162 us  [the longest x1 115 us: program(): pl.pallas_call(functools.partial(mega, sp), out_shape=(out(2, NS, NP, CP)...]
    conv_general_dilated x6 -> x0, matrix products: 136 us -> none  [conv_valid_rows(): lax.conv_general_dilated(inputs, kernel, (stride, stride), ((0, 0), (1, 1...]
    psum x4 -> x0, blocking collectives: 135 us -> none  [the longest x2 71.9 us: band_program(): sums_all = lax.psum(group_sums(mixed_in), 'sp')]
    ppermute x11 -> x0, starting transfers between devices: 33.3 us -> none  [the longest x6 25.6 us: row_from_above(): return lax.ppermute(band_block[:, -1:], 'sp', to_next)]
    convert_element_type x8 -> x0, other arithmetic: 24.9 us -> none  [the longest x4 24.2 us: norm_silu(): jax.nn.silu(values * scale_bc[:, None, None, :] + offset_bc[:, None, None...]
    ppermute x11 -> x0, waiting for transfers between devices: 21.7 us -> none  [the longest x5 21.2 us: row_from_below(): return lax.ppermute(band_block[:, :1], 'sp', to_prev)]
    unnamed x37 -> x2, local copies, waits for them, and re-layouts: 18.6 us -> 0.01 us
  transfers between devices with their start and end apart: 11 -> 0, of which waited for: 7 -> 0; matrix products, arithmetic and copies ran while one was open for 4% -> 0% of each run, Pallas kernels for 0% -> 0%
where the time goes in v1:
time: 172 us; the launch traced here: 171 us
  Pallas kernels  162 us (94%)
  local copies, waits for them, and re-layouts  5.38 us (3%)
  other arithmetic  2.66 us (2%)
    pallas_call x1, Pallas kernels, program(): pl.pallas_call(functools.partial(mega, sp), out_shape=(out(2, NS, NP, CP)...  115 us
    pallas_call x1, Pallas kernels, program(): pl.pallas_call(tail, out_shape=(out(NS, NP, CH),) * 3 + (out(NS, NP // 4,...  47.3 us

profile of v1, /device:TPU:0, one launch (start us, length us, event | category | flops | bytes accessed | tf_op | source)
XLA Modules:
  0.0 171.3 jit_solution(8220772485518921664)
XLA Ops:
  0.6 0.7 reshape.69
  1.3 1.3 reshape.71.bd
  2.6 0.8 reshape.68
  3.4 0.7 pad_maximum_fusion.2.win
  4.1 1.2 slice_bitcast_fusion.1
  5.3 1.3 pad_maximum_fusion
  6.6 0.1 copy.23
  6.7 0.3 reshape.76
  6.9 0.1 pad_slice_fusion.1
  7.1 0.0 copy-start
  7.1 0.1 pad_bitcast_fusion
  7.2 0.7 pad_maximum_fusion.1.edges
  7.8 0.9 pad.26.qx
  8.7 0.0 copy-done
  8.7 115.1 %mega.1 = (bf16[2,16,512,384]{3,2,1,0:T(8,128)(2,1)}, bf16[16,512,320]{2,1,0:T(8,128)(2,1)}, bf16[4,16,64,384]{3,2,1,0:T(8,128)(2,1)}, f32[2,16,384]{2,1,0:T(8,128)}) custom-call(bf16[16,16,512]{2,1,0:T(8,128)(2,1)} %copy-done, bf16[16,16,640]{2,1,0:T(8,128)(2,1)} %pad.26.qx, bf16[2,16,16,128]{3,2,1,0:T(8,128)(2,1)} %pad_maximum_fusion.1.edges, ...), custom_call_target="tpu_custom_call" | custom-call | tf_op jit(solution)/shard_map/mega/pallas_call | solution.py:576
  123.8 47.3 %tail.1 = (bf16[16,512,320]{2,1,0:T(8,128)(2,1)}, bf16[16,512,320]{2,1,0:T(8,128)(2,1)}, bf16[16,512,320]{2,1,0:T(8,128)(2,1)}, bf16[16,128,320]{2,1,0:T(8,128)(2,1)}) custom-call(bf16[2,16,512,384]{3,2,1,0:T(8,128)(2,1)} %get-tuple-element.24.hand, bf16[16,512,320]{2,1,0:T(8,128)(2,1)} %get-tuple-element.25.hand0, ...), custom_call_target="tpu_custom_call" | custom-call | tf_op jit(solution)/shard_map/tail/pallas_call | solution.py:587
  (3 shorter events, 0.0 us)
Async XLA Ops:
  7.1 1.7 copy-start

commit v2 on v1

v2 whole, which is shorter than its diff:
```python
import functools

import jax
import jax.numpy as jnp
from jax import lax
from jax.experimental import pallas as pl
from jax.experimental.pallas import tpu as pltpu
from jax.sharding import PartitionSpec as P

F32, BF = jnp.float32, jnp.bfloat16
GN_GROUPS, GN_EPS = 32, 1e-5
NS, ROWS, ROW, LANE, MAIN = 16, 8, 64, 128, 256
NP = ROWS * ROW
CH = 320
CP = CH + ROW
KP = 4 * MAIN
REST = 3 * MAIN
SPARE = 3 * CH
OFF = 8
GSIZE = CH // GN_GROUPS
PK = ROW + NS
MESH = pl.DeviceIdType.MESH
DUO, TRI, QUAD = range(2), range(3), range(4)
SLOTS = len(QUAD)
NIL = 0.0
ACC32 = dict(preferred_element_type=F32)
ROWS_DOT, COLS_DOT = ((((k,), (k,)), ((), ())) for k in DUO)


def nil(i):
    return jnp.minimum(i, 0) * OFF


def span(i, n=ROW, base=0):
    return slice(base + i * n, base + (i + 1) * n)


def low_half():
    return lax.broadcasted_iota(jnp.int32, (ROW, LANE), 1) < ROW


def widen(p):
    return jnp.concatenate([p, p[..., MAIN:]], -1)


def keep_if(flag, x):
    return jnp.where(jnp.full(x.shape, flag, jnp.int32) > 0, x, NIL)


def store_rest(L, o, r0, r1, r2):
    low = low_half()
    L[span(o), REST:REST + LANE] = jnp.where(low, r0, r1).astype(BF)
    L[span(o), REST + LANE:] = jnp.where(low, r2, 1.0).astype(BF)


def prep_gen(x_of_row, nrows, a, b, L):
    ha, hb = a * 0.5, b * 0.5
    rest = []
    for r in range(nrows + 2):
        x, flag = x_of_row(r)
        h = x.astype(F32) * ha + hb
        n = h + h * jnp.tanh(h)
        if flag is not None:
            n = keep_if(flag, n)
        main = n[:, :MAIN].astype(BF)
        rest.append(n[:, MAIN:])
        for dy in TRI:
            if 0 <= r - dy < nrows:
                L[span(r - dy), span(dy, MAIN)] = main
        if r >= 2:
            store_rest(L, r - 2, *rest[r - 2:])
        yield


def conv_row(Y, o, zero):
    sub = lax.broadcasted_iota(jnp.int32, (OFF, LANE), 0)
    top, bot = sub == 0, sub == 7

    def here(k):
        return Y[k, span(o, base=OFF), :]

    def left(k):
        v = Y[k, pl.ds(zero + (OFF - 1 + o * ROW), ROW), :]
        return jnp.concatenate([jnp.where(top, 0.0, v[:OFF]), v[OFF:]], 0)

    def right(k):
        v = Y[k, pl.ds(zero + (OFF + 1 + o * ROW), ROW), :]
        return jnp.concatenate([v[:-OFF], jnp.where(bot, 0.0, v[-OFF:])], 0)

    out = [left(k) + here(k + 2) + right(k + 4) for k in DUO]
    mix = jnp.where(low_half(), left(6), here(6))
    return out + [mix + pltpu.roll(mix, ROW, 1) + right(7)]


def dot_chunk(L, W, Y, rows, n):
    r = jnp.dot(L[rows, :], W[:, span(n, 2 * MAIN)], **ACC32)
    for k in QUAD:
        Y[4 * n + k, OFF + rows.start:OFF + rows.stop, :] = r[:, span(k, LANE)]


def weave(chunks, gens):
    live = list(gens)
    steps = 0
    for c in chunks:
        c()
        steps += 1
        for _ in range(6):
            for g in list(live):
                if next(g, StopIteration) is StopIteration:
                    live.remove(g)
    for g in live:
        for _ in g:
            pass


def lane_left(x, k):
    return pltpu.roll(x, CP - k, 1)


def starts(k):
    lane = lax.broadcasted_iota(jnp.int32, (OFF, LANE), 1) + k * LANE
    return (lane % GSIZE == 0) & (lane < CH)


def stacked(rows):
    fill = [jnp.zeros((4 - len(rows), rows[0].shape[1]), F32)] * (len(rows) < 4)
    return jnp.concatenate(list(rows) + fill, 0)


def compact(tiles, embs):
    s = stacked([jnp.concatenate([t[k:k + 1] for k in TRI], 1) for t in tiles])
    q = stacked([jnp.concatenate([t[k + 3:k + 4] for k in TRI], 1) for t in tiles])
    e = stacked(embs)
    x = jnp.concatenate([s + float(NP) * e, q + e * (2.0 * s + float(NP) * e)], 0)
    w2 = x + lane_left(x, 1)
    w4 = w2 + lane_left(w2, 2)
    w8 = w4 + lane_left(w4, 4)
    w10 = w8 + lane_left(w2, 8)
    c = sum(jnp.where(starts(k), w10[:, span(k, LANE)], NIL) for k in TRI)
    return [jnp.concatenate([c[k:k + 1], c[k + 4:k + 5]], 0) for k in range(len(tiles))]


def affine(tots, gain, shift, embs, count):
    x = jnp.concatenate([stacked([t[k:k + 1] for t in tots]) for k in DUO], 0)
    y = jnp.concatenate([jnp.where(starts(k), x, NIL) for k in TRI], 1)
    r2 = y + pltpu.roll(y, 1, 1)
    r4 = r2 + pltpu.roll(r2, 2, 1)
    r8 = r4 + pltpu.roll(r4, 4, 1)
    r = r8 + pltpu.roll(r2, 8, 1)
    lane = lax.broadcasted_iota(jnp.int32, (OFF, CP), 1)
    r = jnp.where(lane >= CH, pltpu.roll(r, ROW, 1), r) * (1.0 / count)
    mean, msq = r[:4], r[4:]
    a = gain * lax.rsqrt(msq - mean * mean + GN_EPS)
    return a, shift + a * (stacked(embs) - mean)


def pack_row(dst, x):
    dst[:ROW, :] = jnp.concatenate(x[:2], 1)
    half = ROW // 2
    p = jnp.where(low_half()[:half], x[2][:half].astype(F32), x[2][half:].astype(F32))
    dst[ROW:, :] = jnp.concatenate([p[:NS], p[NS:]], 1).astype(BF)


def unpack_row(src):
    p = src[ROW:, :].astype(F32)
    p = jnp.concatenate([p[:, :LANE], p[:, LANE:]], 0)
    swap, low = pltpu.roll(p, ROW, 1), low_half()[:ROW // 2]
    rest = jnp.concatenate([jnp.where(low, p, swap), jnp.where(low, swap, p)], 0)
    return jnp.concatenate([src[:ROW, :].astype(F32), rest], 1)


def stats_tile(acc, acq):
    parts = [x.sum(0, keepdims=True) for x in acc + acq]
    return jnp.concatenate(parts + [jnp.zeros((2, LANE), F32)], 0)


def add_stats(acc, acq, new):
    for k, x in enumerate(new):
        v = x.astype(F32).reshape(OFF, OFF, LANE)
        acc[k] = acc[k] + v.sum(0)
        acq[k] = acq[k] + (v * v).sum(0)


def no_stats():
    return [jnp.zeros((OFF, LANE), F32) for _ in TRI]


def weight_copies(src, W, WR, sem_main, sem_rest):
    for dy in TRI:
        for dx in TRI:
            cols = span(dx, MAIN)
            pltpu.make_async_copy(src.at[dy, dx, :MAIN, :MAIN], W.at[span(dy, MAIN), cols], sem_main).start()
            pltpu.make_async_copy(src.at[dy, dx, MAIN:, :MAIN], W.at[span(dy, base=REST), cols], sem_main).start()
            pltpu.make_async_copy(src.at[dy, dx, :, MAIN:], WR.at[dy * 3 + dx], sem_rest).start()


def weight_finish(W, WR, bias, sem_main, sem_rest):
    main = W.at[:SPARE, :REST]
    pltpu.make_async_copy(main, main, sem_main).wait()
    pltpu.make_async_copy(WR, WR, sem_rest).wait()
    for dy in TRI:
        for part, rows in ((slice(0, MAIN), span(dy, MAIN)), (slice(MAIN, CH), span(dy, base=REST))):
            w0, w1, w2 = (WR[dy * 3 + dx, part, :] for dx in TRI)
            W[rows, REST:REST + LANE] = jnp.concatenate([w0, w1], 1)
            W[rows, REST + LANE:] = jnp.concatenate([w2, w2], 1)
    b = widen(bias.astype(F32))
    gap = jnp.zeros((1, MAIN), F32)
    rest = jnp.where(low_half()[:1], 0.0, b[:, MAIN:])
    row = jnp.concatenate([gap, b[:, :MAIN], gap, rest, gap[:, :LANE]], 1)
    first = lax.broadcasted_iota(jnp.int32, (ROW, KP), 0) == 0
    W[SPARE:, :] = jnp.where(first, row, NIL).astype(BF)


def mega(sp, q, wi, bi, temb, tb, g1, s1, g2, s2, b1, b2, tw, w1, w2, hand, hand0, halo, abo,
         H, U, H2, HS, W, WR, TW, WI, L0, L1, Y0, Y1, ST, SG, RS, AB, EMB, GAIN, HT, HB, HX, PT, PB, PX, LQ,
         wm_sem, wr_sem, tw_sem, q_send, q_recv, st_send, st_recv, up_send, dn_send, x_send, ht_recv, hb_recv, hx_recv, out_sem, fin_sem):
    me, dp = lax.axis_index("sp"), lax.axis_index("dp")
    has_up, has_dn = (me > 0).astype(jnp.int32), (me < sp - 1).astype(jnp.int32)
    held = (H, U, H2, U)
    last = NS - 1

    get_tw = pltpu.make_async_copy(tw, TW, tw_sem)
    get_tw.start()
    for j, src in enumerate((w1.at[0], w2.at[0], w1.at[1])):
        weight_copies(src, W.at[j], WR.at[j], wm_sem.at[j], wr_sem.at[j])

    barrier = pltpu.get_barrier_semaphore()
    for k in range(1, sp):
        pl.semaphore_signal(barrier, inc=1, device_id=(dp, lax.rem(me + k, sp)), device_id_type=MESH)
    pl.semaphore_wait(barrier, sp - 1)

    def remote(src, dst, ssem, rsem, dev):
        return pltpu.make_async_remote_copy(src_ref=src, dst_ref=dst, send_sem=ssem, recv_sem=rsem, device_id=(dp, dev), device_id_type=MESH)

    def if_up(f):
        pl.when(me > 0)(f)

    def if_dn(f):
        pl.when(me < sp - 1)(f)

    q_dn = remote(q.at[:, :, NP - LANE:], LQ.at[0], q_send.at[0], q_recv.at[0], me + 1)
    q_up = remote(q.at[:, :, :LANE], LQ.at[1], q_send.at[1], q_recv.at[1], me - 1)
    if_dn(q_dn.start)
    if_up(q_up.start)

    def up_copy(slot, s):
        return remote(PT.at[slot - 1, s], HB.at[slot, s], up_send.at[slot, s], hb_recv.at[slot, s], me - 1)

    def dn_copy(slot, s):
        return remote(PB.at[slot - 1, s], HT.at[slot, s], dn_send.at[slot, s], ht_recv.at[slot, s], me + 1)

    def dx_copy(s):
        return remote(PX.at[s], HX.at[s], x_send.at[s], hx_recv.at[s], me + 1)

    def out_copy(slot, s):
        src, dst = ((HS, hand0), None, (H2, hand.at[0]), (U, hand.at[1]))[slot]
        return pltpu.make_async_copy(src.at[s], dst.at[s], out_sem.at[slot, s])

    def send_sums(slot, s):
        for k in range(1, sp):
            remote(SG.at[slot, s], RS.at[slot, s, k - 1], st_send.at[slot, s], st_recv.at[slot, s], lax.rem(me + k, sp)).start()

    def send_rows(slot, s):
        if slot != 1:
            out_copy(slot, s).start()
        if slot == 0:
            return
        if_up(lambda: up_copy(slot, s).start())

        def down():
            dn_copy(slot, s).start()
            if slot == 3:
                dx_copy(s).start()
        if_dn(down)

    def wait_sums(slot, s):
        pltpu.make_async_copy(RS.at[slot, s], RS.at[slot, s], st_recv.at[slot, s]).wait()

    def wait_rows(slot, s):
        if_up(lambda: remote(PB.at[0, s], HT.at[slot, s], dn_send.at[slot, s], ht_recv.at[slot, s], me).wait_recv())
        if_dn(lambda: remote(PT.at[0, s], HB.at[slot, s], up_send.at[slot, s], hb_recv.at[slot, s], me).wait_recv())

    def squeeze(slot, ss):
        rows = compact([ST[slot, s] for s in ss], [EMB[slot, pl.ds(s, 1)] for s in ss])

        def store():
            for r, s in zip(rows, ss):
                SG[slot, s] = r
        return store

    for k, (ref, l) in enumerate(((g1, 0), (g2, 0), (g1, 1), (g2, 1), (s1, 0), (s2, 0), (s1, 1), (s2, 1))):
        GAIN[k:k + 1, :] = widen(ref[l:l + 1, :].astype(F32))
    WI[...] = jnp.zeros_like(WI)
    for dy in TRI:
        for dx in TRI:
            WI[span(4 * dy + dx, 4), :] = widen(wi[dy, dx].astype(F32))
    WI[NS + 12:NS + 13, :] = widen(bi[...].astype(F32))
    get_tw.wait()
    x = temb[...].astype(F32)
    act = (x * jax.nn.sigmoid(x)).astype(BF)
    for l in DUO:
        pr = lax.dot_general(act, TW[l], COLS_DOT, **ACC32)
        EMB[2 * l] = jnp.zeros((NS, CP), F32)
        EMB[2 * l + 1] = widen(pr + tb[l:l + 1, :].astype(F32))

    if_up(q_dn.wait_recv)
    if_dn(q_up.wait_recv)

    def first(s):
        above, below = keep_if(has_up, LQ[0, s].astype(F32)), keep_if(has_dn, LQ[1, s].astype(F32))
        ext = jnp.concatenate([above, q[s].astype(F32), below], 1)
        mid = pltpu.roll(ext, ext.shape[1] - ROW, 1)
        wide = NP + LANE
        lhs = jnp.concatenate([ext[:, :wide], mid[:, :wide], ext[:, LANE:]], 0).astype(BF)
        r = lax.dot_general(lhs, WI[...].astype(BF), ROWS_DOT, **ACC32)
        acc, acq = no_stats(), no_stats()
        for o in range(ROWS + 2):
            x = r[span(o), :].astype(BF)
            parts = [x[:, span(k, LANE)] for k in TRI]
            if o == 0:
                pack_row(HT.at[0, s], parts)
            elif o > ROWS:
                pack_row(HB.at[0, s], parts)
            else:
                H[s, span(o - 1), :] = x
                HS[s, span(o - 1), :] = x[:, :CH]
                add_stats(acc, acq, parts)
        ST[0, s] = stats_tile(acc, acq)

    def first_pair(i, carry):
        t = 2 * i
        for n in (t - 2, t - 1):
            pl.when(i > 0)(functools.partial(send_rows, 0, n))
            pl.when(i > 1)(functools.partial(send_sums, 0, n - 2))
        store = squeeze(0, [lax.rem(n + NS, NS) for n in (t - 2, t - 1)])
        first(t)
        first(t + 1)
        store()
        return carry

    lax.fori_loop(0, NS // 2, first_pair, 0)
    squeeze(0, (last - 1, last))()
    for j in TRI:
        weight_finish(W.at[j], WR.at[j], (b1, b2)[j % 2][j // 2:j // 2 + 1, :], wm_sem.at[j], wr_sem.at[j])
    for s in range(NS - 4, NS):
        send_sums(0, s)
    for s in (last - 1, last):
        send_rows(0, s)

    def scales(slot, ss):
        tots = []
        for s in ss:
            tots.append(SG[slot, s])
            for k in range(sp - 1):
                tots[-1] = tots[-1] + RS[slot, s, k]
        a, b = affine(tots, GAIN[pl.ds(slot, 1)], GAIN[pl.ds(slot + 4, 1)],
                      [EMB[slot, pl.ds(s, 1)] for s in ss], float(sp * NP * GSIZE))

        def store(dst):
            for k, s in enumerate(ss):
                dst[0, pl.ds(s, 1)] = a[k:k + 1]
                dst[1, pl.ds(s, 1)] = b[k:k + 1]
        return store

    def prep_of(slot, s, L, a, b):
        def row(r):
            if r == 0:
                return unpack_row(HT.at[slot, s]), has_up
            if r == ROWS + 1:
                return unpack_row(HB.at[slot, s]), has_dn
            return held[slot][s, span(r - 1), :], None
        return prep_gen(row, ROWS, a, b, L)

    def epi_gen(j, s, Y, zero):
        acc, acq = no_stats(), no_stats()
        edge = {0: PT.at[j, s], ROWS - 1: PB.at[j, s]}
        if j == 2:
            edge[ROWS - 2] = PX.at[s]
        for o in range(ROWS):
            new = [x.astype(BF) for x in conv_row(Y, o, zero)]
            for k in TRI:
                if j == 1:
                    new[k] = (new[k].astype(F32) + H[s, span(o), span(k, LANE)].astype(F32)).astype(BF)
                held[j + 1][s, span(o), span(k, LANE)] = new[k]
            if o in edge:
                pack_row(edge[o], new)
            add_stats(acc, acq, new)
            yield
        ST[j + 1, s] = stats_tile(acc, acq)

    def coeffs(s):
        return AB[0, pl.ds(s, 1)], AB[1, pl.ds(s, 1)]

    def half(j, t, Lc, Ln, Yc, Yp, zero):
        nxt = jnp.minimum(t + 1, last)
        chunks = [functools.partial(dot_chunk, Lc, W.at[j], Yc, slice(0, NP), n) for n in DUO]
        weave(chunks, (prep_of(j, nxt, Ln, *coeffs(nxt)), epi_gen(j, lax.rem(t + last, NS), Yp, zero)))

    for s in QUAD:
        wait_sums(0, s)
    scales(0, QUAD)(AB)
    still = nil(me)
    for _ in prep_of(0, 0, L0, *coeffs(0)):
        pass
    for j in TRI:
        def body(i, carry, j=j):
            t = 2 * i
            zero = nil(i)
            ns = [j * NS + t + k for k in (4, 5)]
            slot = ns[0] // NS
            ss = [lax.rem(n, NS) for n in ns]
            for s in ss:
                if j < 2:
                    wait_sums(slot, s)
                else:
                    pl.when(slot < 3)(functools.partial(wait_sums, slot, s))
            for k in (1, 2):
                if j > 0:
                    wait_rows((j * NS + t + k) // NS, lax.rem(t + k, NS))
                elif k == 2:
                    pl.when(t + k == NS)(lambda: wait_rows(1, 0))
            for n, m in ((t - 2, 0), (t - 3, 1)):
                pl.when(i > m)(functools.partial(send_rows, j + 1, n))
                pl.when(i > m + 1)(functools.partial(send_sums, j + 1, n - 2))
            store = scales(jnp.minimum(slot, 2), ss)
            store_sums = squeeze(j + 1, [lax.rem(t + NS - k, NS) for k in (3, 2)])
            half(j, t, L0, L1, Y0, Y1, zero)
            half(j, t + 1, L1, L0, Y1, Y0, zero)
            store(AB)
            store_sums()
            return carry

        lax.fori_loop(0, NS // 2, body, 0)
        for s in (last - 2, last - 1):
            send_rows(j + 1, s)
            send_sums(j + 1, s - 2)
        squeeze(j + 1, (last - 2, last - 1))()
        for _ in epi_gen(j, last, Y1, still):
            pass
        if j < 2:
            for _ in prep_of(j + 1, 0, L0, *coeffs(0)):
                pass
        squeeze(j + 1, (last,))()
        for s in range(last - 2, NS):
            send_sums(j + 1, s)
        send_rows(j + 1, last)

    def drain(s, carry):
        wait_sums(3, s)
        for slot in QUAD:
            pltpu.make_async_copy(RS.at[slot, s], RS.at[slot, s], st_send.at[slot, s]).wait()
            if slot != 1:
                out_copy(slot, s).wait()
            if slot > 0:
                if_up(lambda slot=slot: up_copy(slot, s).wait_send())
                if_dn(lambda slot=slot: dn_copy(slot, s).wait_send())
        pl.when(s > 0)(lambda: wait_rows(3, s))
        if_up(lambda: dx_copy(s).wait_recv())
        if_dn(lambda: dx_copy(s).wait_send())
        return carry

    lax.fori_loop(0, NS, drain, 0)
    if_dn(q_dn.wait_send)
    if_up(q_up.wait_send)
    fins = [pltpu.make_async_copy(r, halo.at[k], fin_sem.at[k]) for k, r in enumerate((HT.at[2], HT.at[3], HX, HB.at[3]))]
    for f in fins:
        f.start()
    for k in QUAD:
        scales(3, range(4 * k, 4 * k + 4))(abo)
    for f in fins:
        f.wait()


def tail(hand, hand0, halo, ab, b2, bd, w2, dw, h0o, h1o, h2o, do,
         H, U, HA, P0, X2, W, WR, L0, L1, Y0, Y1, O1, O2, OD, DS, in_sem, ha_sem, p_sem, wm_sem, wr_sem, o_sem, od_sem):
    me, sp = lax.axis_index("sp"), lax.axis_size("sp")
    has_up, has_dn = (me > 0).astype(jnp.int32), (me < sp - 1).astype(jnp.int32)

    def gets(s):
        return ([pltpu.make_async_copy(hand.at[k, s], (H, U)[k].at[s], in_sem.at[k, s]) for k in (1, 0)]
                + [pltpu.make_async_copy(halo.at[k, s], HA.at[k, s], ha_sem.at[k, s]) for k in QUAD])

    def take0(s):
        return pltpu.make_async_copy(hand0.at[s], P0.at[s], p_sem.at[s])

    def fetch(s, carry):
        for c in gets(s):
            c.start()
        return carry

    def ready(s):
        for c in gets(s):
            c.wait()

    fetch(0, 0)
    weight_copies(w2.at[1], W.at[0], WR.at[0], wm_sem.at[0], wr_sem.at[0])
    lax.fori_loop(1, 4, fetch, 0)

    def prep_of(s, L):
        def row(r):
            if r < 2:
                return unpack_row(HA.at[2 - r, s]), has_up
            if r == ROWS + 2:
                return unpack_row(HA.at[3, s]), has_dn
            return U[s, span(r - 2), :], None
        return prep_gen(row, ROWS + 1, ab[0, pl.ds(s, 1)], ab[1, pl.ds(s, 1)], L)

    def epi_gen(s, Y, zero):
        for o in range(ROWS + 1):
            t = conv_row(Y, o, zero)
            edge = unpack_row(HA.at[0, s]) if o == 0 else None
            for k in TRI:
                cols = span(k, LANE)
                old = edge[:, cols] if o == 0 else H[s, span(o - 1), cols]
                new = old.astype(F32) + t[k].astype(BF).astype(F32)
                new = (keep_if(has_up, new) if o == 0 else new).astype(BF)
                X2[s, span(o), cols] = new
                if o > 0:
                    n = min(LANE, CH - k * LANE)
                    cols = slice(k * LANE, k * LANE + n)
                    O1[s, span(o - 1), cols] = old[:, :n]
                    O2[s, span(o - 1), cols] = new[:, :n]
            yield

    def put(k, s):
        src, dst = ((P0, h0o), (O1, h1o), (O2, h2o))[k]
        return pltpu.make_async_copy(src.at[s], dst.at[s], o_sem.at[k, s])

    def half(t, Lc, Ln, Yc, Yp, zero):
        chunks = [functools.partial(dot_chunk, Lc, W.at[0], Yc, slice(0, NP + ROW), n) for n in DUO]
        weave(chunks, (prep_of(jnp.minimum(t + 1, NS - 1), Ln), epi_gen(lax.rem(t + NS - 1, NS), Yp, zero)))

    ready(0)
    for _ in prep_of(0, L0):
        pass
    weight_finish(W.at[0], WR.at[0], b2[1:2, :], wm_sem.at[0], wr_sem.at[0])
    weight_copies(dw, W.at[1], WR.at[1], wm_sem.at[1], wr_sem.at[1])

    def body(i, carry):
        t = 2 * i
        zero = nil(i)
        ready(t + 1)
        pl.when(t + 2 < NS)(lambda: ready(t + 2))
        for n in (t, t + 1):
            take0(n).start()
            pl.when(t + 4 < NS)(functools.partial(fetch, n + 4, None))

        @pl.when(i > 0)
        def _():
            for n in (t - 2, t - 1):
                take0(n).wait()
                put(0, n).start()
        for n in (t - 3, t - 2):
            @pl.when(n >= 0)
            def _(n=n):
                put(1, n).start()
                put(2, n).start()
        half(t, L0, L1, Y0, Y1, zero)
        half(t + 1, L1, L0, Y1, Y0, zero)
        return carry

    lax.fori_loop(0, NS // 2, body, 0)
    still = nil(me)
    for _ in epi_gen(NS - 1, Y1, still):
        pass
    for s in range(NS - 3, NS):
        put(1, s).start()
        put(2, s).start()
    for s in (NS - 2, NS - 1):
        take0(s).wait()
        put(0, s).start()
    weight_finish(W.at[1], WR.at[1], bd[...].reshape(1, CH), wm_sem.at[1], wr_sem.at[1])

    def dprep(s, L):
        for o in QUAD:
            xs = [X2[s, span(2 * o + dy), :] for dy in TRI]
            for dy in TRI:
                L[span(o), span(dy, MAIN)] = xs[dy][:, :MAIN]
            store_rest(L, o, *(x[:, MAIN:].astype(F32) for x in xs))

    def depi(s, Y, zero):
        for o in QUAD:
            d = conv_row(Y, o, zero)
            for k in TRI:
                DS[o, k] = d[k]
            parts = [DS[o, k, pl.ds(0, ROW // 2, stride=2), :] for k in TRI]
            OD[s, span(o, ROW // 2), :] = jnp.concatenate(parts, 1)[:, :CH].astype(BF)

    def dhalf(t, Lc, Ln, Yc, Yp, zero):
        for n in DUO:
            dot_chunk(Lc, W.at[1], Yc, slice(0, NP // 2), n)
        dprep(jnp.minimum(t + 1, NS - 1), Ln)
        depi(lax.rem(t + NS - 1, NS), Yp, zero)

    dprep(0, L0)

    def dbody(i, carry):
        t = 2 * i
        zero = nil(i)
        dhalf(t, L0, L1, Y0, Y1, zero)
        dhalf(t + 1, L1, L0, Y1, Y0, zero)
        return carry

    lax.fori_loop(0, NS // 2, dbody, 0)
    depi(NS - 1, Y1, still)
    dout = pltpu.make_async_copy(OD, do, od_sem)
    dout.start()

    def drain(s, carry):
        for k in TRI:
            put(k, s).wait()
        return carry

    lax.fori_loop(0, NS, drain, 0)
    dout.wait()


def solution(mesh):
    sp = mesh.shape["sp"]

    def program(latent, time_emb, w_in, b_in, gn1_scale, gn1_shift, conv1_w, conv1_b, temb_w, temb_b, gn2_scale, gn2_shift, conv2_w, conv2_b, down_w, down_b):
        none = (0, 0)
        lat = jnp.pad(latent.transpose(0, 3, 1, 2), (none, none, none, (1, 1)))
        q = jnp.stack([lat[..., d:d + ROW] for d in TRI], 1).reshape(NS, 12, NP)
        q = jnp.pad(q, (none, (0, 4), none), constant_values=1)

        dma, vm = pltpu.SemaphoreType.DMA, pltpu.VMEM
        any_, vms = pl.BlockSpec(memory_space=pl.ANY), pl.BlockSpec(memory_space=pltpu.VMEM)
        params = functools.partial(pltpu.CompilerParams, vmem_limit_bytes=66_000_000)

        def big(n=NP, c=CP):
            return vm((NS, n, c), BF)

        def edge(n):
            return vm((n, NS, PK, MAIN), BF)

        def bufs(m):
            return [vm((m, KP), BF)] * 2 + [vm((8, m + 2 * OFF, LANE), F32)] * 2

        def out(*shape):
            return jax.ShapeDtypeStruct(shape, BF)

        hand, hand0, halo, ab = pl.pallas_call(
            functools.partial(mega, sp),
            out_shape=(out(2, NS, NP, CP), out(NS, NP, CH), out(SLOTS, NS, PK, MAIN), jax.ShapeDtypeStruct((2, NS, CP), F32)),
            in_specs=[vms] * 11 + [any_] * 3, out_specs=(any_, any_, any_, vms),
            scratch_shapes=[big(), big(), big(), big(NP, CH), vm((3, KP, KP), BF), vm((3, 9, CH, ROW), BF), vm((2, CH, temb_w.shape[1]), BF), vm((3 * NS, CP), F32)] + bufs(NP)
            + [vm((SLOTS, NS, OFF, LANE), F32), vm((SLOTS, NS, 2, LANE), F32), vm((SLOTS, NS, sp - 1, 2, LANE), F32), vm((2, NS, CP), F32), vm((SLOTS, NS, CP), F32), vm((OFF, CP), F32),
               edge(4), edge(4), big(PK, MAIN), edge(3), edge(3), big(PK, MAIN), vm((2, NS, NS, LANE), BF),
               dma((3,)), dma((3,)), dma, dma((2,)), dma((2,)), dma((SLOTS, NS)), dma((SLOTS, NS)), dma((SLOTS, NS)), dma((SLOTS, NS)), dma((NS,)),
               dma((SLOTS, NS)), dma((SLOTS, NS)), dma((NS,)), dma((SLOTS, NS)), dma((4,))],
            compiler_params=params(collective_id=0, has_side_effects=True), name="mega",
        )(q, w_in, b_in.reshape(1, CH), time_emb, temb_b, gn1_scale, gn1_shift, gn2_scale, gn2_shift, conv1_b, conv2_b, temb_w.transpose(0, 2, 1), conv1_w, conv2_w)
        outs = pl.pallas_call(
            tail,
            out_shape=(out(NS, NP, CH),) * 3 + (out(NS, NP // 4, CH),),
            in_specs=[any_] * 3 + [vms] * 3 + [any_] * 2, out_specs=(any_,) * 4,
            scratch_shapes=[big(), big(), edge(4), big(NP, CH), big(NP + ROW), vm((2, KP, KP), BF), vm((2, 9, CH, ROW), BF)] + bufs(NP + ROW)
            + [big(NP, CH), big(NP, CH), big(NP // 4, CH), vm((4, 3, ROW, LANE), F32),
               dma((2, NS)), dma((SLOTS, NS)), dma((NS,)), dma((2,)), dma((2,)), dma((3, NS)), dma],
            compiler_params=params(), name="tail",
        )(hand, hand0, halo, ab, conv2_b, down_b.reshape(1, CH), conv2_w, down_w)
        return tuple(o.reshape(NS, n, m, CH) for o, n, m in zip(outs, [ROWS] * len(TRI) + [ROWS // 2], [ROW] * len(TRI) + [ROW // 2]))

    band = P("dp", "sp", None, None)
    return jax.shard_map(program, mesh=mesh, in_specs=(band, P("dp", None)) + (P(),) * 14, out_specs=(band,) * 4, check_vma=False)
```

time: 172 us -> 154 us (0.90)
  Pallas kernels: 162 us -> 147 us
    pallas_call x1, Pallas kernels: 115 us -> 102 us  [program(): pl.pallas_call(functools.partial(mega, sp), out_shape=(out(2, NS, NP, CP)...]
    pallas_call x1, Pallas kernels: 47.3 us -> 44.4 us  [program(): pl.pallas_call(tail, out_shape=(out(NS, NP, CH),) * 3 + (out(NS, NP // 4,...]
where the time goes in v2:
time: 154 us
  Pallas kernels  147 us (95%)
  local copies, waits for them, and re-layouts  4.79 us (3%)
    pallas_call x1, Pallas kernels, program(): pl.pallas_call(functools.partial(mega, sp), out_shape=(out(2, NS, NP, CP)...  102 us
    pallas_call x1, Pallas kernels, program(): pl.pallas_call(tail, out_shape=(out(NS, NP, CH),) * 3 + (out(NS, NP // 4,...  44.4 us

profile of v2, /device:TPU:0, one launch (start us, length us, event | category | flops | bytes accessed | tf_op | source)
XLA Modules:
  0.0 153.7 jit_solution(1614880737641968737)
XLA Ops:
  0.6 1.2 reshape.30.bi
  1.9 1.3 reshape.31.bd
  3.1 1.2 slice_bitcast_fusion.1
  4.4 1.3 pad_maximum_fusion
  5.6 0.1 copy.23
  5.7 0.3 reshape.36
  6.0 0.7 pad.9.q
  6.7 102.4 %mega.1 = (bf16[2,16,512,384]{3,2,1,0:T(8,128)(2,1)}, bf16[16,512,320]{2,1,0:T(8,128)(2,1)}, bf16[4,16,80,256]{3,2,1,0:T(8,128)(2,1)}, f32[2,16,384]{2,1,0:T(8,128)}) custom-call(bf16[16,16,512]{2,1,0:T(8,128)(2,1)} %pad.9.q, bf16[3,3,4,320]{3,2,1,0:T(4,128)(2,1)} %wi.1, bf16[1,320]{1,0:T(2,128)(2,1)} %reshape.30.bi, bf16[16,1280]{1,0:T(8,128)(2,1)} %temb.1, ...), custom_call_target="tpu_custom_call" | custom-call | tf_op jit(solution)/shard_map/mega/pallas_call | solution.py:643
  109.1 44.4 %tail.1 = (bf16[16,512,320]{2,1,0:T(8,128)(2,1)}, bf16[16,512,320]{2,1,0:T(8,128)(2,1)}, bf16[16,512,320]{2,1,0:T(8,128)(2,1)}, bf16[16,128,320]{2,1,0:T(8,128)(2,1)}) custom-call(bf16[2,16,512,384]{3,2,1,0:T(8,128)(2,1)} %get-tuple-element.12.hand, bf16[16,512,320]{2,1,0:T(8,128)(2,1)} %get-tuple-element.13.hand0, ...), custom_call_target="tpu_custom_call" | custom-call | tf_op jit(solution)/shard_map/tail/pallas_call | solution.py:654

commit v3 on v2

--- a/solution.py
+++ b/solution.py
@@ -23,6 +23,7 @@
 DUO, TRI, QUAD = range(2), range(3), range(4)
 SLOTS = len(QUAD)
 NIL = 0.0
+SHARE = (1, 2, 3, 3)
 ACC32 = dict(preferred_element_type=F32)
 ROWS_DOT, COLS_DOT = ((((k,), (k,)), ((), ())) for k in DUO)
 
@@ -69,7 +70,7 @@
                 L[span(r - dy), span(dy, MAIN)] = main
         if r >= 2:
             store_rest(L, r - 2, *rest[r - 2:])
-        yield
+        yield main
 
 
 def conv_row(Y, o, zero):
@@ -93,22 +94,23 @@
 
 
 def dot_chunk(L, W, Y, rows, n):
-    r = jnp.dot(L[rows, :], W[:, span(n, 2 * MAIN)], **ACC32)
-    for k in QUAD:
-        Y[4 * n + k, OFF + rows.start:OFF + rows.stop, :] = r[:, span(k, LANE)]
-
-
-def weave(chunks, gens):
-    live = list(gens)
-    steps = 0
-    for c in chunks:
-        c()
-        steps += 1
-        for _ in range(6):
-            for g in list(live):
-                if next(g, StopIteration) is StopIteration:
-                    live.remove(g)
-    for g in live:
+    r = jnp.dot(L[rows, :], W[:, span(n, MAIN)], **ACC32)
+    for k in DUO:
+        Y[2 * n + k, OFF + rows.start:OFF + rows.stop, :] = r[:, span(k, LANE)]
+
+
+def weave(L, W, Y, m, prep, epi, share):
+    work = [prep] * (m // ROW + 2) + [epi] * (m // ROW)
+    done = 0
+    for n in QUAD:
+        dot_chunk(L, W, Y, slice(0, m), n)
+        upto = len(work) * share[n] // share[-1]
+        for g in work[done:upto]:
+            mark = next(g)
+        done = upto
+        if n < len(QUAD) - 1:
+            L[:NS, KP - NS:] = jnp.where(mark[:NS, LANE - NS:LANE].astype(F32) > NIL, 1.0, NIL).astype(BF)
+    for g in (prep, epi):
         for _ in g:
             pass
 
@@ -140,7 +142,7 @@
     return [jnp.concatenate([c[k:k + 1], c[k + 4:k + 5]], 0) for k in range(len(tiles))]
 
 
-def affine(tots, gain, shift, embs, count):
+def affine(tots, gains, shifts, embs, count):
     x = jnp.concatenate([stacked([t[k:k + 1] for t in tots]) for k in DUO], 0)
     y = jnp.concatenate([jnp.where(starts(k), x, NIL) for k in TRI], 1)
     r2 = y + pltpu.roll(y, 1, 1)
@@ -150,8 +152,8 @@
     lane = lax.broadcasted_iota(jnp.int32, (OFF, CP), 1)
     r = jnp.where(lane >= CH, pltpu.roll(r, ROW, 1), r) * (1.0 / count)
     mean, msq = r[:4], r[4:]
-    a = gain * lax.rsqrt(msq - mean * mean + GN_EPS)
-    return a, shift + a * (stacked(embs) - mean)
+    a = stacked(gains) * lax.rsqrt(msq - mean * mean + GN_EPS)
+    return a, stacked(shifts) + a * (stacked(embs) - mean)
 
 
 def pack_row(dst, x):
@@ -212,7 +214,7 @@
 
 
 def mega(sp, q, wi, bi, temb, tb, g1, s1, g2, s2, b1, b2, tw, w1, w2, hand, hand0, halo, abo,
-         H, U, H2, HS, W, WR, TW, WI, L0, L1, Y0, Y1, ST, SG, RS, AB, EMB, GAIN, HT, HB, HX, PT, PB, PX, LQ,
+         H, U, H2, HS, W, WR, TW, WI, L0, L1, Y0, Y1, ST, STC, SG, RS, AB, EMB, GAIN, HT, HB, HX, PT, PB, PX, LQ,
          wm_sem, wr_sem, tw_sem, q_send, q_recv, st_send, st_recv, up_send, dn_send, x_send, ht_recv, hb_recv, hx_recv, out_sem, fin_sem):
     me, dp = lax.axis_index("sp"), lax.axis_index("dp")
     has_up, has_dn = (me > 0).astype(jnp.int32), (me < sp - 1).astype(jnp.int32)
@@ -280,13 +282,9 @@
         if_up(lambda: remote(PB.at[0, s], HT.at[slot, s], dn_send.at[slot, s], ht_recv.at[slot, s], me).wait_recv())
         if_dn(lambda: remote(PT.at[0, s], HB.at[slot, s], up_send.at[slot, s], hb_recv.at[slot, s], me).wait_recv())
 
-    def squeeze(slot, ss):
-        rows = compact([ST[slot, s] for s in ss], [EMB[slot, pl.ds(s, 1)] for s in ss])
-
-        def store():
-            for r, s in zip(rows, ss):
-                SG[slot, s] = r
-        return store
+    def squeeze(slot, ss, tiles):
+        for r, s in zip(compact(tiles, [EMB[slot, pl.ds(s, 1)] for s in ss]), ss):
+            SG[slot, s] = r
 
     for k, (ref, l) in enumerate(((g1, 0), (g2, 0), (g1, 1), (g2, 1), (s1, 0), (s2, 0), (s1, 1), (s2, 1))):
         GAIN[k:k + 1, :] = widen(ref[l:l + 1, :].astype(F32))
@@ -294,7 +292,7 @@
     for dy in TRI:
         for dx in TRI:
             WI[span(4 * dy + dx, 4), :] = widen(wi[dy, dx].astype(F32))
-    WI[NS + 12:NS + 13, :] = widen(bi[...].astype(F32))
+    WI[NS + 12:NS + 13, :] = widen(bi[...].reshape(1, CH).astype(F32))
     get_tw.wait()
     x = temb[...].astype(F32)
     act = (x * jax.nn.sigmoid(x)).astype(BF)
@@ -325,21 +323,22 @@
                 H[s, span(o - 1), :] = x
                 HS[s, span(o - 1), :] = x[:, :CH]
                 add_stats(acc, acq, parts)
-        ST[0, s] = stats_tile(acc, acq)
+        ST[s] = stats_tile(acc, acq)
 
     def first_pair(i, carry):
         t = 2 * i
         for n in (t - 2, t - 1):
             pl.when(i > 0)(functools.partial(send_rows, 0, n))
             pl.when(i > 1)(functools.partial(send_sums, 0, n - 2))
-        store = squeeze(0, [lax.rem(n + NS, NS) for n in (t - 2, t - 1)])
+        ss = [lax.rem(n + NS, NS) for n in (t - 2, t - 1)]
+        tiles = [ST[s] for s in ss]
         first(t)
         first(t + 1)
-        store()
+        squeeze(0, ss, tiles)
         return carry
 
     lax.fori_loop(0, NS // 2, first_pair, 0)
-    squeeze(0, (last - 1, last))()
+    squeeze(0, (last - 1, last), (ST[last - 1], ST[last]))
     for j in TRI:
         weight_finish(W.at[j], WR.at[j], (b1, b2)[j % 2][j // 2:j // 2 + 1, :], wm_sem.at[j], wr_sem.at[j])
     for s in range(NS - 4, NS):
@@ -347,20 +346,14 @@
     for s in (last - 1, last):
         send_rows(0, s)
 
-    def scales(slot, ss):
+    def scales(slots, ss):
         tots = []
-        for s in ss:
+        for slot, s in zip(slots, ss):
             tots.append(SG[slot, s])
             for k in range(sp - 1):
                 tots[-1] = tots[-1] + RS[slot, s, k]
-        a, b = affine(tots, GAIN[pl.ds(slot, 1)], GAIN[pl.ds(slot + 4, 1)],
-                      [EMB[slot, pl.ds(s, 1)] for s in ss], float(sp * NP * GSIZE))
-
-        def store(dst):
-            for k, s in enumerate(ss):
-                dst[0, pl.ds(s, 1)] = a[k:k + 1]
-                dst[1, pl.ds(s, 1)] = b[k:k + 1]
-        return store
+        return affine(tots, [GAIN[pl.ds(k, 1)] for k in slots], [GAIN[pl.ds(k + SLOTS, 1)] for k in slots],
+                      [EMB[k, pl.ds(s, 1)] for k, s in zip(slots, ss)], float(sp * NP * GSIZE))
 
     def prep_of(slot, s, L, a, b):
         def row(r):
@@ -371,13 +364,14 @@
             return held[slot][s, span(r - 1), :], None
         return prep_gen(row, ROWS, a, b, L)
 
-    def epi_gen(j, s, Y, zero):
+    def epi_gen(j, s, Y, zero, tiles):
         acc, acq = no_stats(), no_stats()
         edge = {0: PT.at[j, s], ROWS - 1: PB.at[j, s]}
         if j == 2:
             edge[ROWS - 2] = PX.at[s]
         for o in range(ROWS):
             new = [x.astype(BF) for x in conv_row(Y, o, zero)]
+            mark = new[2]
             for k in TRI:
                 if j == 1:
                     new[k] = (new[k].astype(F32) + H[s, span(o), span(k, LANE)].astype(F32)).astype(BF)
@@ -385,64 +379,67 @@
             if o in edge:
                 pack_row(edge[o], new)
             add_stats(acc, acq, new)
-            yield
-        ST[j + 1, s] = stats_tile(acc, acq)
-
-    def coeffs(s):
-        return AB[0, pl.ds(s, 1)], AB[1, pl.ds(s, 1)]
-
-    def half(j, t, Lc, Ln, Yc, Yp, zero):
-        nxt = jnp.minimum(t + 1, last)
-        chunks = [functools.partial(dot_chunk, Lc, W.at[j], Yc, slice(0, NP), n) for n in DUO]
-        weave(chunks, (prep_of(j, nxt, Ln, *coeffs(nxt)), epi_gen(j, lax.rem(t + last, NS), Yp, zero)))
-
-    for s in QUAD:
+            if o == ROWS - 1:
+                tiles.append(stats_tile(acc, acq))
+            yield mark
+
+    for Y in (Y0, Y1):
+        Y[...] = jnp.zeros_like(Y)
+    for s in TRI:
         wait_sums(0, s)
-    scales(0, QUAD)(AB)
+    for c, v in enumerate(scales((0,) * 3, TRI)):
+        AB[c] = v[:3]
     still = nil(me)
-    for _ in prep_of(0, 0, L0, *coeffs(0)):
+    ahead = len(QUAD)
+    for _ in prep_of(0, 0, L0, AB[0, :1], AB[1, :1]):
         pass
     for j in TRI:
         def body(i, carry, j=j):
-            t = 2 * i
+            t = ahead * i
             zero = nil(i)
-            ns = [j * NS + t + k for k in (4, 5)]
-            slot = ns[0] // NS
-            ss = [lax.rem(n, NS) for n in ns]
-            for s in ss:
+            ns = [jnp.minimum(j * NS + t + 3 + k, 3 * NS - 1) for k in QUAD]
+            for k, n in enumerate(ns):
+                go = functools.partial(wait_sums, n // NS, lax.rem(n, NS))
                 if j < 2:
-                    wait_sums(slot, s)
+                    go()
                 else:
-                    pl.when(slot < 3)(functools.partial(wait_sums, slot, s))
-            for k in (1, 2):
+                    pl.when(t + 3 + k < NS)(go)
+            for k in QUAD:
                 if j > 0:
-                    wait_rows((j * NS + t + k) // NS, lax.rem(t + k, NS))
-                elif k == 2:
-                    pl.when(t + k == NS)(lambda: wait_rows(1, 0))
-            for n, m in ((t - 2, 0), (t - 3, 1)):
-                pl.when(i > m)(functools.partial(send_rows, j + 1, n))
-                pl.when(i > m + 1)(functools.partial(send_sums, j + 1, n - 2))
-            store = scales(jnp.minimum(slot, 2), ss)
-            store_sums = squeeze(j + 1, [lax.rem(t + NS - k, NS) for k in (3, 2)])
-            half(j, t, L0, L1, Y0, Y1, zero)
-            half(j, t + 1, L1, L0, Y1, Y0, zero)
-            store(AB)
-            store_sums()
+                    wait_rows((j * NS + t + k + 1) // NS, lax.rem(t + k + 1, NS))
+                elif k == ahead - 1:
+                    pl.when(t + ahead == NS)(lambda: wait_rows(1, 0))
+            for k in QUAD:
+                pl.when(t + k > ahead)(functools.partial(send_rows, j + 1, t + k - 5))
+                pl.when(t + k > ahead + 1)(functools.partial(send_sums, j + 1, t + k - 6))
+            a, b = scales([n // NS for n in ns], [lax.rem(n, NS) for n in ns])
+            co = [(AB[0, k:k + 1], AB[1, k:k + 1]) for k in (1, 2)] + [(a[k:k + 1], b[k:k + 1]) for k in DUO]
+            tiles = [STC[...]]
+            for u in QUAD:
+                nxt = jnp.minimum(t + u + 1, last)
+                if u % 2:
+                    Lc, Ln, Yc, Yp = L1, L0, Y1, Y0
+                else:
+                    Lc, Ln, Yc, Yp = L0, L1, Y0, Y1
+                weave(Lc, W.at[j], Yc, NP, prep_of(j, nxt, Ln, *co[u]), epi_gen(j, lax.rem(t + u + last, NS), Yp, zero, tiles), SHARE)
+            AB[0], AB[1] = a[1:], b[1:]
+            STC[...] = tiles.pop()
+            squeeze(j + 1, [lax.rem(t + last - 1 + k, NS) for k in QUAD], tiles)
             return carry
 
-        lax.fori_loop(0, NS // 2, body, 0)
-        for s in (last - 2, last - 1):
-            send_rows(j + 1, s)
-            send_sums(j + 1, s - 2)
-        squeeze(j + 1, (last - 2, last - 1))()
-        for _ in epi_gen(j, last, Y1, still):
+        lax.fori_loop(0, NS // ahead, body, 0)
+        for k in QUAD:
+            send_rows(j + 1, last - ahead + k)
+            send_sums(j + 1, last - ahead - 1 + k)
+        tiles = [STC[...]]
+        for _ in epi_gen(j, last, Y1, still, tiles):
             pass
         if j < 2:
-            for _ in prep_of(j + 1, 0, L0, *coeffs(0)):
+            for _ in prep_of(j + 1, 0, L0, AB[0, :1], AB[1, :1]):
                 pass
-        squeeze(j + 1, (last,))()
-        for s in range(last - 2, NS):
-            send_sums(j + 1, s)
+        squeeze(j + 1, (last - 1, last), tiles)
+        send_sums(j + 1, last - 1)
+        send_sums(j + 1, last)
         send_rows(j + 1, last)
 
     def drain(s, carry):
@@ -466,7 +463,8 @@
     for f in fins:
         f.start()
     for k in QUAD:
-        scales(3, range(4 * k, 4 * k + 4))(abo)
+        for c, v in enumerate(scales((3,) * ahead, range(ahead * k, ahead * k + ahead))):
+            abo[c, span(k, ahead)] = v
     for f in fins:
         f.wait()
 
@@ -494,7 +492,7 @@
 
     fetch(0, 0)
     weight_copies(w2.at[1], W.at[0], WR.at[0], wm_sem.at[0], wr_sem.at[0])
-    lax.fori_loop(1, 4, fetch, 0)
+    lax.fori_loop(1, len(QUAD) + 1, fetch, 0)
 
     def prep_of(s, L):
         def row(r):
@@ -507,12 +505,12 @@
 
     def epi_gen(s, Y, zero):
         for o in range(ROWS + 1):
-            t = conv_row(Y, o, zero)
+            t = [x.astype(BF) for x in conv_row(Y, o, zero)]
             edge = unpack_row(HA.at[0, s]) if o == 0 else None
             for k in TRI:
                 cols = span(k, LANE)
                 old = edge[:, cols] if o == 0 else H[s, span(o - 1), cols]
-                new = old.astype(F32) + t[k].astype(BF).astype(F32)
+                new = old.astype(F32) + t[k].astype(F32)
                 new = (keep_if(has_up, new) if o == 0 else new).astype(BF)
                 X2[s, span(o), cols] = new
                 if o > 0:
@@ -520,15 +518,11 @@
                     cols = slice(k * LANE, k * LANE + n)
                     O1[s, span(o - 1), cols] = old[:, :n]
                     O2[s, span(o - 1), cols] = new[:, :n]
-            yield
+            yield t[2]
 
     def put(k, s):
         src, dst = ((P0, h0o), (O1, h1o), (O2, h2o))[k]
         return pltpu.make_async_copy(src.at[s], dst.at[s], o_sem.at[k, s])
-
-    def half(t, Lc, Ln, Yc, Yp, zero):
-        chunks = [functools.partial(dot_chunk, Lc, W.at[0], Yc, slice(0, NP + ROW), n) for n in DUO]
-        weave(chunks, (prep_of(jnp.minimum(t + 1, NS - 1), Ln), epi_gen(lax.rem(t + NS - 1, NS), Yp, zero)))
 
     ready(0)
     for _ in prep_of(0, L0):
@@ -536,37 +530,45 @@
     weight_finish(W.at[0], WR.at[0], b2[1:2, :], wm_sem.at[0], wr_sem.at[0])
     weight_copies(dw, W.at[1], WR.at[1], wm_sem.at[1], wr_sem.at[1])
 
+    for Y in (Y0, Y1):
+        Y[...] = jnp.zeros_like(Y)
+    ahead = len(QUAD)
+
     def body(i, carry):
-        t = 2 * i
+        t = ahead * i
         zero = nil(i)
-        ready(t + 1)
-        pl.when(t + 2 < NS)(lambda: ready(t + 2))
-        for n in (t, t + 1):
-            take0(n).start()
-            pl.when(t + 4 < NS)(functools.partial(fetch, n + 4, None))
+        for k in QUAD:
+            pl.when(t + k + 1 < NS)(functools.partial(ready, t + k + 1))
+            pl.when(t + k + ahead + 1 < NS)(functools.partial(fetch, t + k + ahead + 1, None))
+            take0(t + k).start()
 
         @pl.when(i > 0)
         def _():
-            for n in (t - 2, t - 1):
-                take0(n).wait()
-                put(0, n).start()
-        for n in (t - 3, t - 2):
-            @pl.when(n >= 0)
-            def _(n=n):
+            for k in QUAD:
+                take0(t - ahead + k).wait()
+                put(0, t - ahead + k).start()
+
+        for k in QUAD:
+            @pl.when(t + k > ahead)
+            def _(n=t + k - 5):
                 put(1, n).start()
                 put(2, n).start()
-        half(t, L0, L1, Y0, Y1, zero)
-        half(t + 1, L1, L0, Y1, Y0, zero)
+        for u in QUAD:
+            if u % 2:
+                Lc, Ln, Yc, Yp = L1, L0, Y1, Y0
+            else:
+                Lc, Ln, Yc, Yp = L0, L1, Y0, Y1
+            weave(Lc, W.at[0], Yc, NP + ROW, prep_of(jnp.minimum(t + u + 1, NS - 1), Ln), epi_gen(lax.rem(t + u + NS - 1, NS), Yp, zero), SHARE)
         return carry
 
-    lax.fori_loop(0, NS // 2, body, 0)
+    lax.fori_loop(0, NS // ahead, body, 0)
     still = nil(me)
     for _ in epi_gen(NS - 1, Y1, still):
         pass
-    for s in range(NS - 3, NS):
+    for s in range(NS - ahead - 1, NS):
         put(1, s).start()
         put(2, s).start()
-    for s in (NS - 2, NS - 1):
+    for s in range(NS - ahead, NS):
         take0(s).wait()
         put(0, s).start()
     weight_finish(W.at[1], WR.at[1], bd[...].reshape(1, CH), wm_sem.at[1], wr_sem.at[1])
@@ -587,7 +589,7 @@
             OD[s, span(o, ROW // 2), :] = jnp.concatenate(parts, 1)[:, :CH].astype(BF)
 
     def dhalf(t, Lc, Ln, Yc, Yp, zero):
-        for n in DUO:
+        for n in QUAD:
             dot_chunk(Lc, W.at[1], Yc, slice(0, NP // 2), n)
         dprep(jnp.minimum(t + 1, NS - 1), Ln)
         depi(lax.rem(t + NS - 1, NS), Yp, zero)
@@ -645,12 +647,12 @@
             out_shape=(out(2, NS, NP, CP), out(NS, NP, CH), out(SLOTS, NS, PK, MAIN), jax.ShapeDtypeStruct((2, NS, CP), F32)),
             in_specs=[vms] * 11 + [any_] * 3, out_specs=(any_, any_, any_, vms),
             scratch_shapes=[big(), big(), big(), big(NP, CH), vm((3, KP, KP), BF), vm((3, 9, CH, ROW), BF), vm((2, CH, temb_w.shape[1]), BF), vm((3 * NS, CP), F32)] + bufs(NP)
-            + [vm((SLOTS, NS, OFF, LANE), F32), vm((SLOTS, NS, 2, LANE), F32), vm((SLOTS, NS, sp - 1, 2, LANE), F32), vm((2, NS, CP), F32), vm((SLOTS, NS, CP), F32), vm((OFF, CP), F32),
+            + [vm((NS, OFF, LANE), F32), vm((OFF, LANE), F32), vm((SLOTS, NS, 2, LANE), F32), vm((SLOTS, NS, sp - 1, 2, LANE), F32), vm((2, 3, CP), F32), vm((SLOTS, NS, CP), F32), vm((OFF, CP), F32),
                edge(4), edge(4), big(PK, MAIN), edge(3), edge(3), big(PK, MAIN), vm((2, NS, NS, LANE), BF),
                dma((3,)), dma((3,)), dma, dma((2,)), dma((2,)), dma((SLOTS, NS)), dma((SLOTS, NS)), dma((SLOTS, NS)), dma((SLOTS, NS)), dma((NS,)),
                dma((SLOTS, NS)), dma((SLOTS, NS)), dma((NS,)), dma((SLOTS, NS)), dma((4,))],
             compiler_params=params(collective_id=0, has_side_effects=True), name="mega",
-        )(q, w_in, b_in.reshape(1, CH), time_emb, temb_b, gn1_scale, gn1_shift, gn2_scale, gn2_shift, conv1_b, conv2_b, temb_w.transpose(0, 2, 1), conv1_w, conv2_w)
+        )(q, w_in, b_in, time_emb, temb_b, gn1_scale, gn1_shift, gn2_scale, gn2_shift, conv1_b, conv2_b, temb_w.transpose(0, 2, 1), conv1_w, conv2_w)
         outs = pl.pallas_call(
             tail,
             out_shape=(out(NS, NP, CH),) * 3 + (out(NS, NP // 4, CH),),
@@ -659,7 +661,7 @@
             + [big(NP, CH), big(NP, CH), big(NP // 4, CH), vm((4, 3, ROW, LANE), F32),
                dma((2, NS)), dma((SLOTS, NS)), dma((NS,)), dma((2,)), dma((2,)), dma((3, NS)), dma],
             compiler_params=params(), name="tail",
-        )(hand, hand0, halo, ab, conv2_b, down_b.reshape(1, CH), conv2_w, down_w)
+        )(hand, hand0, halo, ab, conv2_b, down_b, conv2_w, down_w)
         return tuple(o.reshape(NS, n, m, CH) for o, n, m in zip(outs, [ROWS] * len(TRI) + [ROWS // 2], [ROW] * len(TRI) + [ROW // 2]))
 
     band = P("dp", "sp", None, None)

time: 154 us -> 153 us (level)
  local copies, waits for them, and re-layouts: 4.79 us -> 2.3 us
    reshape x2 -> x0, local copies, waits for them, and re-layouts: 2.5 us -> none  [the longest x1 1.25 us: program(): down_b.reshape(1, CH)]
where the time goes in v3:
time: 153 us; the launch traced here: 152 us
  Pallas kernels  148 us (97%)
  local copies, waits for them, and re-layouts  2.3 us (2%)
    pallas_call x1, Pallas kernels, program(): pl.pallas_call(functools.partial(mega, sp), out_shape=(out(2, NS, NP, CP)...  104 us
    pallas_call x1, Pallas kernels, program(): pl.pallas_call(tail, out_shape=(out(NS, NP, CH),) * 3 + (out(NS, NP // 4,...  44.4 us

profile of v3, /device:TPU:0, one launch (start us, length us, event | category | flops | bytes accessed | tf_op | source)
XLA Modules:
  0.0 152.3 jit_solution(4291680800774169110)
XLA Ops:
  0.6 1.2 slice_bitcast_fusion.1
  1.9 1.3 pad_maximum_fusion
  3.1 0.1 copy.23
  3.2 0.3 reshape.28
  3.5 0.7 pad.9.q
  4.2 103.5 %mega.1 = (bf16[2,16,512,384]{3,2,1,0:T(8,128)(2,1)}, bf16[16,512,320]{2,1,0:T(8,128)(2,1)}, bf16[4,16,80,256]{3,2,1,0:T(8,128)(2,1)}, f32[2,16,384]{2,1,0:T(8,128)}) custom-call(bf16[16,16,512]{2,1,0:T(8,128)(2,1)} %pad.9.q, bf16[3,3,4,320]{3,2,1,0:T(4,128)(2,1)} %wi.1, bf16[320]{0:T(512)(128)(2,1)} %bi.1, bf16[16,1280]{1,0:T(8,128)(2,1)} %temb.1, ...), custom_call_target="tpu_custom_call" | custom-call | tf_op jit(solution)/shard_map/mega/pallas_call | solution.py:645
  107.8 44.4 %tail.1 = (bf16[16,512,320]{2,1,0:T(8,128)(2,1)}, bf16[16,512,320]{2,1,0:T(8,128)(2,1)}, bf16[16,512,320]{2,1,0:T(8,128)(2,1)}, bf16[16,128,320]{2,1,0:T(8,128)(2,1)}) custom-call(bf16[2,16,512,384]{3,2,1,0:T(8,128)(2,1)} %get-tuple-element.12.hand, bf16[16,512,320]{2,1,0:T(8,128)(2,1)} %get-tuple-element.13.hand0, ...), custom_call_target="tpu_custom_call" | custom-call | tf_op jit(solution)/shard_map/tail/pallas_call | solution.py:656

commit v4 on v3

--- a/solution.py
+++ b/solution.py
@@ -23,6 +23,14 @@
 DUO, TRI, QUAD = range(2), range(3), range(4)
 SLOTS = len(QUAD)
 NIL = 0.0
+
+
+def groups(n, step):
+    cuts = [0, *range(n, NS, step), NS]
+    return [(a, b - a) for a, b in zip(cuts, cuts[1:])]
+
+
+SUMS, EDGES = groups(2, SLOTS), groups(3, SLOTS)
 SHARE = (1, 2, 3, 3)
 ACC32 = dict(preferred_element_type=F32)
 ROWS_DOT, COLS_DOT = ((((k,), (k,)), ((), ())) for k in DUO)
@@ -196,7 +204,7 @@
             pltpu.make_async_copy(src.at[dy, dx, :, MAIN:], WR.at[dy * 3 + dx], sem_rest).start()
 
 
-def weight_finish(W, WR, bias, sem_main, sem_rest):
+def weight_finish(bias, W, WR, sem_main, sem_rest):
     main = W.at[:SPARE, :REST]
     pltpu.make_async_copy(main, main, sem_main).wait()
     pltpu.make_async_copy(WR, WR, sem_rest).wait()
@@ -245,48 +253,49 @@
     if_dn(q_dn.start)
     if_up(q_up.start)
 
-    def up_copy(slot, s):
-        return remote(PT.at[slot - 1, s], HB.at[slot, s], up_send.at[slot, s], hb_recv.at[slot, s], me - 1)
-
-    def dn_copy(slot, s):
-        return remote(PB.at[slot - 1, s], HT.at[slot, s], dn_send.at[slot, s], ht_recv.at[slot, s], me + 1)
-
-    def dx_copy(s):
-        return remote(PX.at[s], HX.at[s], x_send.at[s], hx_recv.at[s], me + 1)
-
-    def out_copy(slot, s):
+    def rows_copies(slot, g, lo, n):
+        ss = pl.ds(lo, n)
+        up = remote(PT.at[slot - 1, ss], HB.at[slot, ss], up_send.at[slot, g], hb_recv.at[slot, g], me - 1)
+        down = [remote(PB.at[slot - 1, ss], HT.at[slot, ss], dn_send.at[slot, g], ht_recv.at[slot, g], me + 1)]
+        if slot == 3:
+            down.append(remote(PX.at[ss], HX.at[ss], x_send.at[g], hx_recv.at[g], me + 1))
+        return up, down
+
+    def out_copy(slot, g, lo, n):
         src, dst = ((HS, hand0), None, (H2, hand.at[0]), (U, hand.at[1]))[slot]
-        return pltpu.make_async_copy(src.at[s], dst.at[s], out_sem.at[slot, s])
-
-    def send_sums(slot, s):
+        ss = pl.ds(lo, n)
+        return pltpu.make_async_copy(src.at[ss], dst.at[ss], out_sem.at[slot, g])
+
+    def send_sums(slot, g, lo, n):
+        ss = pl.ds(lo, n)
         for k in range(1, sp):
-            remote(SG.at[slot, s], RS.at[slot, s, k - 1], st_send.at[slot, s], st_recv.at[slot, s], lax.rem(me + k, sp)).start()
-
-    def send_rows(slot, s):
+            remote(SG.at[slot, ss], RS.at[slot, k - 1, ss], st_send.at[slot, g], st_recv.at[slot, g], lax.rem(me + k, sp)).start()
+
+    def send_rows(slot, g, lo, n):
         if slot != 1:
-            out_copy(slot, s).start()
-        if slot == 0:
-            return
-        if_up(lambda: up_copy(slot, s).start())
-
-        def down():
-            dn_copy(slot, s).start()
-            if slot == 3:
-                dx_copy(s).start()
-        if_dn(down)
-
-    def wait_sums(slot, s):
-        pltpu.make_async_copy(RS.at[slot, s], RS.at[slot, s], st_recv.at[slot, s]).wait()
-
-    def wait_rows(slot, s):
-        if_up(lambda: remote(PB.at[0, s], HT.at[slot, s], dn_send.at[slot, s], ht_recv.at[slot, s], me).wait_recv())
-        if_dn(lambda: remote(PT.at[0, s], HB.at[slot, s], up_send.at[slot, s], hb_recv.at[slot, s], me).wait_recv())
+            out_copy(slot, g, lo, n).start()
+        if slot > 0:
+            up, down = rows_copies(slot, g, lo, n)
+            if_up(up.start)
+            if_dn(lambda: [c.start() for c in down] and None)
+
+    def sums_bytes(slot, n, sem, g):
+        both = RS.at[slot, :, :n]
+        return pltpu.make_async_copy(both, both, sem.at[slot, g])
+
+    def wait_sums(slot, g, n):
+        sums_bytes(slot, n, st_recv, g).wait()
+
+    def wait_rows(slot, g, n):
+        ss = pl.ds(0, n)
+        if_up(lambda: remote(PB.at[0, ss], HT.at[slot, ss], dn_send.at[slot, g], ht_recv.at[slot, g], me).wait_recv())
+        if_dn(lambda: remote(PT.at[0, ss], HB.at[slot, ss], up_send.at[slot, g], hb_recv.at[slot, g], me).wait_recv())
 
     def squeeze(slot, ss, tiles):
         for r, s in zip(compact(tiles, [EMB[slot, pl.ds(s, 1)] for s in ss]), ss):
             SG[slot, s] = r
 
-    for k, (ref, l) in enumerate(((g1, 0), (g2, 0), (g1, 1), (g2, 1), (s1, 0), (s2, 0), (s1, 1), (s2, 1))):
+    for k, (ref, l) in enumerate((ref, l) for pair in ((g1, g2), (s1, s2)) for l in DUO for ref in pair):
         GAIN[k:k + 1, :] = widen(ref[l:l + 1, :].astype(F32))
     WI[...] = jnp.zeros_like(WI)
     for dy in TRI:
@@ -327,9 +336,9 @@
 
     def first_pair(i, carry):
         t = 2 * i
-        for n in (t - 2, t - 1):
-            pl.when(i > 0)(functools.partial(send_rows, 0, n))
-            pl.when(i > 1)(functools.partial(send_sums, 0, n - 2))
+        for g in TRI:
+            for parts, send in ((EDGES, send_rows), (SUMS, send_sums)):
+                pl.when(i == 2 * g + 2)(functools.partial(send, 0, g, *parts[g]))
         ss = [lax.rem(n + NS, NS) for n in (t - 2, t - 1)]
         tiles = [ST[s] for s in ss]
         first(t)
@@ -340,18 +349,17 @@
     lax.fori_loop(0, NS // 2, first_pair, 0)
     squeeze(0, (last - 1, last), (ST[last - 1], ST[last]))
     for j in TRI:
-        weight_finish(W.at[j], WR.at[j], (b1, b2)[j % 2][j // 2:j // 2 + 1, :], wm_sem.at[j], wr_sem.at[j])
-    for s in range(NS - 4, NS):
-        send_sums(0, s)
-    for s in (last - 1, last):
-        send_rows(0, s)
+        weight_finish((b1, b2)[j % 2][j // 2:j // 2 + 1, :], W.at[j], WR.at[j], wm_sem.at[j], wr_sem.at[j])
+    for g in (3, 4):
+        send_sums(0, g, *SUMS[g])
+        send_rows(0, g, *EDGES[g])
 
     def scales(slots, ss):
         tots = []
         for slot, s in zip(slots, ss):
             tots.append(SG[slot, s])
             for k in range(sp - 1):
-                tots[-1] = tots[-1] + RS[slot, s, k]
+                tots[-1] = tots[-1] + RS[slot, k, s]
         return affine(tots, [GAIN[pl.ds(k, 1)] for k in slots], [GAIN[pl.ds(k + SLOTS, 1)] for k in slots],
                       [EMB[k, pl.ds(s, 1)] for k, s in zip(slots, ss)], float(sp * NP * GSIZE))
 
@@ -385,8 +393,8 @@
 
     for Y in (Y0, Y1):
         Y[...] = jnp.zeros_like(Y)
-    for s in TRI:
-        wait_sums(0, s)
+    for g in DUO:
+        wait_sums(0, g, SUMS[g][1])
     for c, v in enumerate(scales((0,) * 3, TRI)):
         AB[c] = v[:3]
     still = nil(me)
@@ -398,20 +406,19 @@
             t = ahead * i
             zero = nil(i)
             ns = [jnp.minimum(j * NS + t + 3 + k, 3 * NS - 1) for k in QUAD]
-            for k, n in enumerate(ns):
-                go = functools.partial(wait_sums, n // NS, lax.rem(n, NS))
+            turn = ahead - 1
+            for g in TRI:
+                pl.when(i == g)(functools.partial(wait_sums, j, g + 2, SUMS[g + 2][1]))
+            for g in DUO:
                 if j < 2:
-                    go()
-                else:
-                    pl.when(t + 3 + k < NS)(go)
-            for k in QUAD:
-                if j > 0:
-                    wait_rows((j * NS + t + k + 1) // NS, lax.rem(t + k + 1, NS))
-                elif k == ahead - 1:
-                    pl.when(t + ahead == NS)(lambda: wait_rows(1, 0))
-            for k in QUAD:
-                pl.when(t + k > ahead)(functools.partial(send_rows, j + 1, t + k - 5))
-                pl.when(t + k > ahead + 1)(functools.partial(send_sums, j + 1, t + k - 6))
+                    pl.when(i == turn)(functools.partial(wait_sums, j + 1, g, SUMS[g][1]))
+            if j > 0:
+                pl.when(i < turn)(lambda: wait_rows(j, i + 1, ahead))
+                pl.when(i == turn)(lambda: wait_rows(j, ahead, 1))
+            pl.when(i == turn)(lambda: wait_rows(j + 1, 0, EDGES[0][1]))
+            for parts, send in ((EDGES, send_rows), (SUMS, send_sums)):
+                for g in TRI:
+                    pl.when(i == g + 1)(functools.partial(send, j + 1, g, *parts[g]))
             a, b = scales([n // NS for n in ns], [lax.rem(n, NS) for n in ns])
             co = [(AB[0, k:k + 1], AB[1, k:k + 1]) for k in (1, 2)] + [(a[k:k + 1], b[k:k + 1]) for k in DUO]
             tiles = [STC[...]]
@@ -428,9 +435,8 @@
             return carry
 
         lax.fori_loop(0, NS // ahead, body, 0)
-        for k in QUAD:
-            send_rows(j + 1, last - ahead + k)
-            send_sums(j + 1, last - ahead - 1 + k)
+        send_rows(j + 1, 3, *EDGES[3])
+        send_sums(j + 1, 3, *SUMS[3])
         tiles = [STC[...]]
         for _ in epi_gen(j, last, Y1, still, tiles):
             pass
@@ -438,25 +444,22 @@
             for _ in prep_of(j + 1, 0, L0, AB[0, :1], AB[1, :1]):
                 pass
         squeeze(j + 1, (last - 1, last), tiles)
-        send_sums(j + 1, last - 1)
-        send_sums(j + 1, last)
-        send_rows(j + 1, last)
-
-    def drain(s, carry):
-        wait_sums(3, s)
+        send_sums(j + 1, 4, *SUMS[4])
+        send_rows(j + 1, 4, *EDGES[4])
+
+    for g in range(len(SUMS)):
+        wait_sums(3, g, SUMS[g][1])
+        if g > 0:
+            wait_rows(3, g, EDGES[g][1])
         for slot in QUAD:
-            pltpu.make_async_copy(RS.at[slot, s], RS.at[slot, s], st_send.at[slot, s]).wait()
+            sums_bytes(slot, SUMS[g][1], st_send, g).wait()
             if slot != 1:
-                out_copy(slot, s).wait()
+                out_copy(slot, g, *EDGES[g]).wait()
             if slot > 0:
-                if_up(lambda slot=slot: up_copy(slot, s).wait_send())
-                if_dn(lambda slot=slot: dn_copy(slot, s).wait_send())
-        pl.when(s > 0)(lambda: wait_rows(3, s))
-        if_up(lambda: dx_copy(s).wait_recv())
-        if_dn(lambda: dx_copy(s).wait_send())
-        return carry
-
-    lax.fori_loop(0, NS, drain, 0)
+                up, down = rows_copies(slot, g, *EDGES[g])
+                if_up(up.wait_send)
+                if_dn(lambda down=down: [c.wait_send() for c in down] and None)
+        if_up(rows_copies(3, g, *EDGES[g])[1][1].wait_recv)
     if_dn(q_dn.wait_send)
     if_up(q_up.wait_send)
     fins = [pltpu.make_async_copy(r, halo.at[k], fin_sem.at[k]) for k, r in enumerate((HT.at[2], HT.at[3], HX, HB.at[3]))]
@@ -491,7 +494,8 @@
             c.wait()
 
     fetch(0, 0)
-    weight_copies(w2.at[1], W.at[0], WR.at[0], wm_sem.at[0], wr_sem.at[0])
+    parts = [(W.at[j], WR.at[j], wm_sem.at[j], wr_sem.at[j]) for j in DUO]
+    weight_copies(w2.at[1], *parts[0])
     lax.fori_loop(1, len(QUAD) + 1, fetch, 0)
 
     def prep_of(s, L):
@@ -527,8 +531,8 @@
     ready(0)
     for _ in prep_of(0, L0):
         pass
-    weight_finish(W.at[0], WR.at[0], b2[1:2, :], wm_sem.at[0], wr_sem.at[0])
-    weight_copies(dw, W.at[1], WR.at[1], wm_sem.at[1], wr_sem.at[1])
+    weight_finish(b2[1:2, :], *parts[0])
+    weight_copies(dw, *parts[1])
 
     for Y in (Y0, Y1):
         Y[...] = jnp.zeros_like(Y)
@@ -571,7 +575,7 @@
     for s in range(NS - ahead, NS):
         take0(s).wait()
         put(0, s).start()
-    weight_finish(W.at[1], WR.at[1], bd[...].reshape(1, CH), wm_sem.at[1], wr_sem.at[1])
+    weight_finish(bd[...].reshape(1, CH), *parts[1])
 
     def dprep(s, L):
         for o in QUAD:
@@ -647,10 +651,10 @@
             out_shape=(out(2, NS, NP, CP), out(NS, NP, CH), out(SLOTS, NS, PK, MAIN), jax.ShapeDtypeStruct((2, NS, CP), F32)),
             in_specs=[vms] * 11 + [any_] * 3, out_specs=(any_, any_, any_, vms),
             scratch_shapes=[big(), big(), big(), big(NP, CH), vm((3, KP, KP), BF), vm((3, 9, CH, ROW), BF), vm((2, CH, temb_w.shape[1]), BF), vm((3 * NS, CP), F32)] + bufs(NP)
-            + [vm((NS, OFF, LANE), F32), vm((OFF, LANE), F32), vm((SLOTS, NS, 2, LANE), F32), vm((SLOTS, NS, sp - 1, 2, LANE), F32), vm((2, 3, CP), F32), vm((SLOTS, NS, CP), F32), vm((OFF, CP), F32),
+            + [vm((NS, OFF, LANE), F32), vm((OFF, LANE), F32), vm((SLOTS, NS, 2, LANE), F32), vm((SLOTS, sp - 1, NS, 2, LANE), F32), vm((2, 3, CP), F32), vm((SLOTS, NS, CP), F32), vm((OFF, CP), F32),
                edge(4), edge(4), big(PK, MAIN), edge(3), edge(3), big(PK, MAIN), vm((2, NS, NS, LANE), BF),
-               dma((3,)), dma((3,)), dma, dma((2,)), dma((2,)), dma((SLOTS, NS)), dma((SLOTS, NS)), dma((SLOTS, NS)), dma((SLOTS, NS)), dma((NS,)),
-               dma((SLOTS, NS)), dma((SLOTS, NS)), dma((NS,)), dma((SLOTS, NS)), dma((4,))],
+               dma((3,)), dma((3,)), dma] + [dma((2,))] * 2 + [dma((SLOTS, len(SUMS)))] * SLOTS + [dma((len(SUMS),))]
+            + [dma((SLOTS, len(SUMS)))] * 2 + [dma((len(SUMS),)), dma((SLOTS, len(SUMS))), dma((4,))],
             compiler_params=params(collective_id=0, has_side_effects=True), name="mega",
         )(q, w_in, b_in, time_emb, temb_b, gn1_scale, gn1_shift, gn2_scale, gn2_shift, conv1_b, conv2_b, temb_w.transpose(0, 2, 1), conv1_w, conv2_w)
         outs = pl.pallas_call(

time: 153 us -> 149 us (0.974)
  Pallas kernels: 148 us -> 144 us
    pallas_call x1, Pallas kernels: 104 us -> 99.8 us  [program(): pl.pallas_call(functools.partial(mega, sp), out_shape=(out(2, NS, NP, CP)...]
where the time goes in v4:
time: 149 us
  Pallas kernels  144 us (97%)
  local copies, waits for them, and re-layouts  2.3 us (2%)
    pallas_call x1, Pallas kernels, program(): pl.pallas_call(functools.partial(mega, sp), out_shape=(out(2, NS, NP, CP)...  99.8 us
    pallas_call x1, Pallas kernels, program(): pl.pallas_call(tail, out_shape=(out(NS, NP, CH),) * 3 + (out(NS, NP // 4,...  44.4 us

profile of v4, /device:TPU:0, one launch (start us, length us, event | category | flops | bytes accessed | tf_op | source)
XLA Modules:
  0.0 148.6 jit_solution(14498106393771864031)
XLA Ops:
  0.6 1.2 slice_bitcast_fusion.1
  1.9 1.3 pad_maximum_fusion
  3.1 0.1 copy.23
  3.2 0.3 reshape.28
  3.5 0.7 pad.9.q
  4.2 99.8 %mega.1 = (bf16[2,16,512,384]{3,2,1,0:T(8,128)(2,1)}, bf16[16,512,320]{2,1,0:T(8,128)(2,1)}, bf16[4,16,80,256]{3,2,1,0:T(8,128)(2,1)}, f32[2,16,384]{2,1,0:T(8,128)}) custom-call(bf16[16,16,512]{2,1,0:T(8,128)(2,1)} %pad.9.q, bf16[3,3,4,320]{3,2,1,0:T(4,128)(2,1)} %wi.1, bf16[320]{0:T(512)(128)(2,1)} %bi.1, bf16[16,1280]{1,0:T(8,128)(2,1)} %temb.1, ...), custom_call_target="tpu_custom_call" | custom-call | tf_op jit(solution)/shard_map/mega/pallas_call | solution.py:649
  104.0 44.4 %tail.1 = (bf16[16,512,320]{2,1,0:T(8,128)(2,1)}, bf16[16,512,320]{2,1,0:T(8,128)(2,1)}, bf16[16,512,320]{2,1,0:T(8,128)(2,1)}, bf16[16,128,320]{2,1,0:T(8,128)(2,1)}) custom-call(bf16[2,16,512,384]{3,2,1,0:T(8,128)(2,1)} %get-tuple-element.12.hand, bf16[16,512,320]{2,1,0:T(8,128)(2,1)} %get-tuple-element.13.hand0, ...), custom_call_target="tpu_custom_call" | custom-call | tf_op jit(solution)/shard_map/tail/pallas_call | solution.py:660

commit v5 on v4

--- a/solution.py
+++ b/solution.py
@@ -81,24 +81,25 @@
         yield main
 
 
+def shifted(v, step):
+    v = pltpu.roll(v.reshape(OFF, OFF, LANE), step % OFF, 1)
+    sub = lax.broadcasted_iota(jnp.int32, v.shape, 1)
+    gap = jnp.zeros_like(v[:1])
+    if step > 0:
+        v = jnp.where(sub == 0, jnp.concatenate([gap, v[:-1]], 0), v)
+    else:
+        v = jnp.where(sub == OFF - 1, jnp.concatenate([v[1:], gap], 0), v)
+    return v.reshape(ROW, LANE)
+
+
 def conv_row(Y, o, zero):
-    sub = lax.broadcasted_iota(jnp.int32, (OFF, LANE), 0)
-    top, bot = sub == 0, sub == 7
-
     def here(k):
         return Y[k, span(o, base=OFF), :]
 
-    def left(k):
-        v = Y[k, pl.ds(zero + (OFF - 1 + o * ROW), ROW), :]
-        return jnp.concatenate([jnp.where(top, 0.0, v[:OFF]), v[OFF:]], 0)
-
-    def right(k):
-        v = Y[k, pl.ds(zero + (OFF + 1 + o * ROW), ROW), :]
-        return jnp.concatenate([v[:-OFF], jnp.where(bot, 0.0, v[-OFF:])], 0)
-
-    out = [left(k) + here(k + 2) + right(k + 4) for k in DUO]
-    mix = jnp.where(low_half(), left(6), here(6))
-    return out + [mix + pltpu.roll(mix, ROW, 1) + right(7)]
+    out = [shifted(here(k), 1) + here(k + 2) + shifted(here(k + 4), -1) for k in DUO]
+    a = here(6)
+    mix = jnp.where(low_half(), shifted(a, 1), a)
+    return out + [mix + pltpu.roll(mix, ROW, 1) + shifted(here(7), -1)]
 
 
 def dot_chunk(L, W, Y, rows, n):

time: 149 us -> 147 us (0.987)
  Pallas kernels: 144 us -> 142 us
where the time goes in v5:
time: 147 us
  Pallas kernels  142 us (97%)
  local copies, waits for them, and re-layouts  2.3 us (2%)
    pallas_call x1, Pallas kernels, program(): pl.pallas_call(functools.partial(mega, sp), out_shape=(out(2, NS, NP, CP)...  99.3 us
    pallas_call x1, Pallas kernels, program(): pl.pallas_call(tail, out_shape=(out(NS, NP, CH),) * 3 + (out(NS, NP // 4,...  43 us

profile of v5, /device:TPU:0, one launch (start us, length us, event | category | flops | bytes accessed | tf_op | source)
XLA Modules:
  0.0 146.7 jit_solution(16651989494820436788)
XLA Ops:
  0.6 1.2 slice_bitcast_fusion.1
  1.9 1.3 pad_maximum_fusion
  3.1 0.1 copy.23
  3.2 0.3 reshape.28
  3.5 0.7 pad.9.q
  4.2 99.3 %mega.1 = (bf16[2,16,512,384]{3,2,1,0:T(8,128)(2,1)}, bf16[16,512,320]{2,1,0:T(8,128)(2,1)}, bf16[4,16,80,256]{3,2,1,0:T(8,128)(2,1)}, f32[2,16,384]{2,1,0:T(8,128)}) custom-call(bf16[16,16,512]{2,1,0:T(8,128)(2,1)} %pad.9.q, bf16[3,3,4,320]{3,2,1,0:T(4,128)(2,1)} %wi.1, bf16[320]{0:T(512)(128)(2,1)} %bi.1, bf16[16,1280]{1,0:T(8,128)(2,1)} %temb.1, ...), custom_call_target="tpu_custom_call" | custom-call | tf_op jit(solution)/shard_map/mega/pallas_call | solution.py:650
  103.5 43.0 %tail.1 = (bf16[16,512,320]{2,1,0:T(8,128)(2,1)}, bf16[16,512,320]{2,1,0:T(8,128)(2,1)}, bf16[16,512,320]{2,1,0:T(8,128)(2,1)}, bf16[16,128,320]{2,1,0:T(8,128)(2,1)}) custom-call(bf16[2,16,512,384]{3,2,1,0:T(8,128)(2,1)} %get-tuple-element.12.hand, bf16[16,512,320]{2,1,0:T(8,128)(2,1)} %get-tuple-element.13.hand0, ...), custom_call_target="tpu_custom_call" | custom-call | tf_op jit(solution)/shard_map/tail/pallas_call | solution.py:661

commit v6 on v5

--- a/solution.py
+++ b/solution.py
@@ -222,17 +222,18 @@
     W[SPARE:, :] = jnp.where(first, row, NIL).astype(BF)
 
 
-def mega(sp, q, wi, bi, temb, tb, g1, s1, g2, s2, b1, b2, tw, w1, w2, hand, hand0, halo, abo,
-         H, U, H2, HS, W, WR, TW, WI, L0, L1, Y0, Y1, ST, STC, SG, RS, AB, EMB, GAIN, HT, HB, HX, PT, PB, PX, LQ,
-         wm_sem, wr_sem, tw_sem, q_send, q_recv, st_send, st_recv, up_send, dn_send, x_send, ht_recv, hb_recv, hx_recv, out_sem, fin_sem):
+def mega(sp, q, wi, bi, temb, tb, g1, s1, g2, s2, b1, b2, tw, w1, w2, hand, halo,
+         H, U, H2, HS, W, WR, TW, WI, L0, L1, Y0, Y1, ST, STC, SG, RS, AB, EMB, GAIN, HT, HB, PT, PB, LQ,
+         wm_sem, wr_sem, tw_sem, q_send, q_recv, st_send, st_recv, up_send, dn_send, ht_recv, hb_recv, out_sem, fin_sem):
     me, dp = lax.axis_index("sp"), lax.axis_index("dp")
     has_up, has_dn = (me > 0).astype(jnp.int32), (me < sp - 1).astype(jnp.int32)
     held = (H, U, H2, U)
+    end = SLOTS
     last = NS - 1
 
     get_tw = pltpu.make_async_copy(tw, TW, tw_sem)
     get_tw.start()
-    for j, src in enumerate((w1.at[0], w2.at[0], w1.at[1])):
+    for j, src in enumerate((w1.at[0], w2.at[0], w1.at[1], w2.at[1])):
         weight_copies(src, W.at[j], WR.at[j], wm_sem.at[j], wr_sem.at[j])
 
     barrier = pltpu.get_barrier_semaphore()
@@ -256,16 +257,14 @@
 
     def rows_copies(slot, g, lo, n):
         ss = pl.ds(lo, n)
-        up = remote(PT.at[slot - 1, ss], HB.at[slot, ss], up_send.at[slot, g], hb_recv.at[slot, g], me - 1)
-        down = [remote(PB.at[slot - 1, ss], HT.at[slot, ss], dn_send.at[slot, g], ht_recv.at[slot, g], me + 1)]
-        if slot == 3:
-            down.append(remote(PX.at[ss], HX.at[ss], x_send.at[g], hx_recv.at[g], me + 1))
-        return up, down
+        down = remote(PB.at[slot - 1, ss], HT.at[slot, ss], dn_send.at[slot, g], ht_recv.at[slot, g], me + 1)
+        if slot == end:
+            return None, down
+        return remote(PT.at[slot - 1, ss], HB.at[slot, ss], up_send.at[slot, g], hb_recv.at[slot, g], me - 1), down
 
     def out_copy(slot, g, lo, n):
-        src, dst = ((HS, hand0), None, (H2, hand.at[0]), (U, hand.at[1]))[slot]
         ss = pl.ds(lo, n)
-        return pltpu.make_async_copy(src.at[ss], dst.at[ss], out_sem.at[slot, g])
+        return pltpu.make_async_copy(HS.at[ss], hand.at[slot // 2, ss], out_sem.at[slot, g])
 
     def send_sums(slot, g, lo, n):
         ss = pl.ds(lo, n)
@@ -273,12 +272,13 @@
             remote(SG.at[slot, ss], RS.at[slot, k - 1, ss], st_send.at[slot, g], st_recv.at[slot, g], lax.rem(me + k, sp)).start()
 
     def send_rows(slot, g, lo, n):
-        if slot != 1:
+        if slot % 2 == 0:
             out_copy(slot, g, lo, n).start()
         if slot > 0:
             up, down = rows_copies(slot, g, lo, n)
-            if_up(up.start)
-            if_dn(lambda: [c.start() for c in down] and None)
+            if up is not None:
+                if_up(up.start)
+            if_dn(down.start)
 
     def sums_bytes(slot, n, sem, g):
         both = RS.at[slot, :, :n]
@@ -290,7 +290,8 @@
     def wait_rows(slot, g, n):
         ss = pl.ds(0, n)
         if_up(lambda: remote(PB.at[0, ss], HT.at[slot, ss], dn_send.at[slot, g], ht_recv.at[slot, g], me).wait_recv())
-        if_dn(lambda: remote(PT.at[0, ss], HB.at[slot, ss], up_send.at[slot, g], hb_recv.at[slot, g], me).wait_recv())
+        if slot is not end:
+            if_dn(lambda: remote(PT.at[0, ss], HB.at[slot, ss], up_send.at[slot, g], hb_recv.at[slot, g], me).wait_recv())
 
     def squeeze(slot, ss, tiles):
         for r, s in zip(compact(tiles, [EMB[slot, pl.ds(s, 1)] for s in ss]), ss):
@@ -349,7 +350,7 @@
 
     lax.fori_loop(0, NS // 2, first_pair, 0)
     squeeze(0, (last - 1, last), (ST[last - 1], ST[last]))
-    for j in TRI:
+    for j in QUAD:
         weight_finish((b1, b2)[j % 2][j // 2:j // 2 + 1, :], W.at[j], WR.at[j], wm_sem.at[j], wr_sem.at[j])
     for g in (3, 4):
         send_sums(0, g, *SUMS[g])
@@ -375,19 +376,24 @@
 
     def epi_gen(j, s, Y, zero, tiles):
         acc, acq = no_stats(), no_stats()
-        edge = {0: PT.at[j, s], ROWS - 1: PB.at[j, s]}
-        if j == 2:
-            edge[ROWS - 2] = PX.at[s]
+        edge = {ROWS - 1: PB.at[j, s]}
+        if j + 1 < end:
+            edge[0] = PT.at[j, s]
         for o in range(ROWS):
             new = [x.astype(BF) for x in conv_row(Y, o, zero)]
             mark = new[2]
             for k in TRI:
-                if j == 1:
-                    new[k] = (new[k].astype(F32) + H[s, span(o), span(k, LANE)].astype(F32)).astype(BF)
-                held[j + 1][s, span(o), span(k, LANE)] = new[k]
+                cols = span(k, LANE)
+                if j % 2:
+                    new[k] = (new[k].astype(F32) + held[j - 1][s, span(o), cols].astype(F32)).astype(BF)
+                    cols_out = slice(k * LANE, min(k * LANE + LANE, CH))
+                    HS[s, span(o), cols_out] = new[k][:, :cols_out.stop - cols_out.start]
+                if j + 1 < end:
+                    held[j + 1][s, span(o), cols] = new[k]
             if o in edge:
                 pack_row(edge[o], new)
-            add_stats(acc, acq, new)
+            if j + 1 < end:
+                add_stats(acc, acq, new)
             if o == ROWS - 1:
                 tiles.append(stats_tile(acc, acq))
             yield mark
@@ -399,191 +405,117 @@
     for c, v in enumerate(scales((0,) * 3, TRI)):
         AB[c] = v[:3]
     still = nil(me)
-    ahead = len(QUAD)
     for _ in prep_of(0, 0, L0, AB[0, :1], AB[1, :1]):
         pass
-    for j in TRI:
+    for j in QUAD:
+        if j % 2:
+            for g in range(len(EDGES)):
+                out_copy(j - 1, g, *EDGES[g]).wait()
+
         def body(i, carry, j=j):
-            t = ahead * i
+            t = 2 * i
             zero = nil(i)
-            ns = [jnp.minimum(j * NS + t + 3 + k, 3 * NS - 1) for k in QUAD]
-            turn = ahead - 1
+            turn = NS // 2 - 1
+            ns = [jnp.minimum(j * NS + t + 3 + k, end * NS - 1) for k in DUO]
             for g in TRI:
-                pl.when(i == g)(functools.partial(wait_sums, j, g + 2, SUMS[g + 2][1]))
+                pl.when(i == 2 * g + 1)(functools.partial(wait_sums, j, g + 2, SUMS[g + 2][1]))
             for g in DUO:
-                if j < 2:
-                    pl.when(i == turn)(functools.partial(wait_sums, j + 1, g, SUMS[g][1]))
+                if j + 1 < end:
+                    pl.when(i == turn - 1 + g)(functools.partial(wait_sums, j + 1, g, SUMS[g][1]))
             if j > 0:
-                pl.when(i < turn)(lambda: wait_rows(j, i + 1, ahead))
-                pl.when(i == turn)(lambda: wait_rows(j, ahead, 1))
-            pl.when(i == turn)(lambda: wait_rows(j + 1, 0, EDGES[0][1]))
-            for parts, send in ((EDGES, send_rows), (SUMS, send_sums)):
                 for g in TRI:
-                    pl.when(i == g + 1)(functools.partial(send, j + 1, g, *parts[g]))
-            a, b = scales([n // NS for n in ns], [lax.rem(n, NS) for n in ns])
-            co = [(AB[0, k:k + 1], AB[1, k:k + 1]) for k in (1, 2)] + [(a[k:k + 1], b[k:k + 1]) for k in DUO]
+                    pl.when(i == 2 * g + 1)(functools.partial(wait_rows, j, g + 1, EDGES[g + 1][1]))
+                pl.when(i == turn)(functools.partial(wait_rows, j, 4, EDGES[4][1]))
+            if j + 1 < end:
+                pl.when(i == turn)(functools.partial(wait_rows, j + 1, 0, EDGES[0][1]))
+            for parts, send in ((EDGES, send_rows), (SUMS, send_sums))[:end - j]:
+                for g in TRI:
+                    pl.when(i == 2 * g + 2)(functools.partial(send, j + 1, g, *parts[g]))
+            new = scales([n // NS for n in ns], [lax.rem(n, NS) for n in ns])
+            co = [(AB[0, k:k + 1], AB[1, k:k + 1]) for k in (1, 2)]
             tiles = [STC[...]]
-            for u in QUAD:
+            for u, (Lc, Ln, Yc, Yp) in enumerate(((L0, L1, Y0, Y1), (L1, L0, Y1, Y0))):
                 nxt = jnp.minimum(t + u + 1, last)
-                if u % 2:
-                    Lc, Ln, Yc, Yp = L1, L0, Y1, Y0
-                else:
-                    Lc, Ln, Yc, Yp = L0, L1, Y0, Y1
                 weave(Lc, W.at[j], Yc, NP, prep_of(j, nxt, Ln, *co[u]), epi_gen(j, lax.rem(t + u + last, NS), Yp, zero, tiles), SHARE)
-            AB[0], AB[1] = a[1:], b[1:]
+            for c in DUO:
+                AB[c] = jnp.concatenate([co[1][c], new[c][:2]], 0)
+            if j + 1 == end:
+                return carry
             STC[...] = tiles.pop()
-            squeeze(j + 1, [lax.rem(t + last - 1 + k, NS) for k in QUAD], tiles)
+            squeeze(j + 1, [lax.rem(t + last - 1 + k, NS) for k in DUO], tiles)
             return carry
 
-        lax.fori_loop(0, NS // ahead, body, 0)
+        lax.fori_loop(0, NS // 2, body, 0)
         send_rows(j + 1, 3, *EDGES[3])
-        send_sums(j + 1, 3, *SUMS[3])
+        if j + 1 < end:
+            send_sums(j + 1, 3, *SUMS[3])
         tiles = [STC[...]]
         for _ in epi_gen(j, last, Y1, still, tiles):
             pass
-        if j < 2:
+        if j + 1 < end:
             for _ in prep_of(j + 1, 0, L0, AB[0, :1], AB[1, :1]):
                 pass
-        squeeze(j + 1, (last - 1, last), tiles)
-        send_sums(j + 1, 4, *SUMS[4])
+            squeeze(j + 1, (last - 1, last), tiles)
+            send_sums(j + 1, 4, *SUMS[4])
         send_rows(j + 1, 4, *EDGES[4])
 
     for g in range(len(SUMS)):
-        wait_sums(3, g, SUMS[g][1])
-        if g > 0:
-            wait_rows(3, g, EDGES[g][1])
+        wait_rows(end, g, EDGES[g][1])
+        out_copy(end, g, *EDGES[g]).wait()
         for slot in QUAD:
             sums_bytes(slot, SUMS[g][1], st_send, g).wait()
-            if slot != 1:
-                out_copy(slot, g, *EDGES[g]).wait()
-            if slot > 0:
-                up, down = rows_copies(slot, g, *EDGES[g])
+            up, down = rows_copies(slot + 1, g, *EDGES[g])
+            if up is not None:
                 if_up(up.wait_send)
-                if_dn(lambda down=down: [c.wait_send() for c in down] and None)
-        if_up(rows_copies(3, g, *EDGES[g])[1][1].wait_recv)
+            if_dn(down.wait_send)
     if_dn(q_dn.wait_send)
     if_up(q_up.wait_send)
-    fins = [pltpu.make_async_copy(r, halo.at[k], fin_sem.at[k]) for k, r in enumerate((HT.at[2], HT.at[3], HX, HB.at[3]))]
-    for f in fins:
-        f.start()
-    for k in QUAD:
-        for c, v in enumerate(scales((3,) * ahead, range(ahead * k, ahead * k + ahead))):
-            abo[c, span(k, ahead)] = v
-    for f in fins:
-        f.wait()
-
-
-def tail(hand, hand0, halo, ab, b2, bd, w2, dw, h0o, h1o, h2o, do,
-         H, U, HA, P0, X2, W, WR, L0, L1, Y0, Y1, O1, O2, OD, DS, in_sem, ha_sem, p_sem, wm_sem, wr_sem, o_sem, od_sem):
-    me, sp = lax.axis_index("sp"), lax.axis_size("sp")
-    has_up, has_dn = (me > 0).astype(jnp.int32), (me < sp - 1).astype(jnp.int32)
-
-    def gets(s):
-        return ([pltpu.make_async_copy(hand.at[k, s], (H, U)[k].at[s], in_sem.at[k, s]) for k in (1, 0)]
-                + [pltpu.make_async_copy(halo.at[k, s], HA.at[k, s], ha_sem.at[k, s]) for k in QUAD])
-
-    def take0(s):
-        return pltpu.make_async_copy(hand0.at[s], P0.at[s], p_sem.at[s])
-
-    def fetch(s, carry):
-        for c in gets(s):
-            c.start()
-        return carry
-
-    def ready(s):
-        for c in gets(s):
-            c.wait()
-
-    fetch(0, 0)
-    parts = [(W.at[j], WR.at[j], wm_sem.at[j], wr_sem.at[j]) for j in DUO]
-    weight_copies(w2.at[1], *parts[0])
-    lax.fori_loop(1, len(QUAD) + 1, fetch, 0)
-
-    def prep_of(s, L):
-        def row(r):
-            if r < 2:
-                return unpack_row(HA.at[2 - r, s]), has_up
-            if r == ROWS + 2:
-                return unpack_row(HA.at[3, s]), has_dn
-            return U[s, span(r - 2), :], None
-        return prep_gen(row, ROWS + 1, ab[0, pl.ds(s, 1)], ab[1, pl.ds(s, 1)], L)
-
-    def epi_gen(s, Y, zero):
-        for o in range(ROWS + 1):
-            t = [x.astype(BF) for x in conv_row(Y, o, zero)]
-            edge = unpack_row(HA.at[0, s]) if o == 0 else None
-            for k in TRI:
-                cols = span(k, LANE)
-                old = edge[:, cols] if o == 0 else H[s, span(o - 1), cols]
-                new = old.astype(F32) + t[k].astype(F32)
-                new = (keep_if(has_up, new) if o == 0 else new).astype(BF)
-                X2[s, span(o), cols] = new
-                if o > 0:
-                    n = min(LANE, CH - k * LANE)
-                    cols = slice(k * LANE, k * LANE + n)
-                    O1[s, span(o - 1), cols] = old[:, :n]
-                    O2[s, span(o - 1), cols] = new[:, :n]
-            yield t[2]
+    fin = pltpu.make_async_copy(HT.at[end], halo, fin_sem)
+    fin.start()
+    fin.wait()
+
+
+def tail(hand, halo, bd, dw, h0o, h1o, h2o, do, P0, P1, P2, HA, W, WR, L0, L1, Y0, Y1, OD, DS, in_sem, ha_sem, wm_sem, wr_sem, o_sem, od_sem):
+    me = lax.axis_index("sp")
+    has_up = (me > 0).astype(jnp.int32)
+    held, outs = (P0, P1, P2), (h0o, h1o, h2o)
+    ahead = len(QUAD)
+
+    def take(k, s):
+        return pltpu.make_async_copy(hand.at[k, s], held[k].at[s], in_sem.at[k, s])
 
     def put(k, s):
-        src, dst = ((P0, h0o), (O1, h1o), (O2, h2o))[k]
-        return pltpu.make_async_copy(src.at[s], dst.at[s], o_sem.at[k, s])
-
-    ready(0)
-    for _ in prep_of(0, L0):
-        pass
-    weight_finish(b2[1:2, :], *parts[0])
-    weight_copies(dw, *parts[1])
-
+        return pltpu.make_async_copy(held[k].at[s], outs[k].at[s], o_sem.at[k, s])
+
+    def fetch(s):
+        for k in (2, 0, 1):
+            take(k, s).start()
+
+    get_halo = pltpu.make_async_copy(halo, HA, ha_sem)
+    take(2, 0).start()
+    get_halo.start()
+    weight_copies(dw, W, WR, wm_sem, wr_sem)
+    for k in DUO:
+        take(k, 0).start()
+    for s in range(1, ahead):
+        fetch(s)
     for Y in (Y0, Y1):
         Y[...] = jnp.zeros_like(Y)
-    ahead = len(QUAD)
-
-    def body(i, carry):
-        t = ahead * i
-        zero = nil(i)
-        for k in QUAD:
-            pl.when(t + k + 1 < NS)(functools.partial(ready, t + k + 1))
-            pl.when(t + k + ahead + 1 < NS)(functools.partial(fetch, t + k + ahead + 1, None))
-            take0(t + k).start()
-
-        @pl.when(i > 0)
-        def _():
-            for k in QUAD:
-                take0(t - ahead + k).wait()
-                put(0, t - ahead + k).start()
-
-        for k in QUAD:
-            @pl.when(t + k > ahead)
-            def _(n=t + k - 5):
-                put(1, n).start()
-                put(2, n).start()
-        for u in QUAD:
-            if u % 2:
-                Lc, Ln, Yc, Yp = L1, L0, Y1, Y0
-            else:
-                Lc, Ln, Yc, Yp = L0, L1, Y0, Y1
-            weave(Lc, W.at[0], Yc, NP + ROW, prep_of(jnp.minimum(t + u + 1, NS - 1), Ln), epi_gen(lax.rem(t + u + NS - 1, NS), Yp, zero), SHARE)
-        return carry
-
-    lax.fori_loop(0, NS // ahead, body, 0)
+    get_halo.wait()
+    take(2, 0).wait()
     still = nil(me)
-    for _ in epi_gen(NS - 1, Y1, still):
-        pass
-    for s in range(NS - ahead - 1, NS):
-        put(1, s).start()
-        put(2, s).start()
-    for s in range(NS - ahead, NS):
-        take0(s).wait()
-        put(0, s).start()
-    weight_finish(bd[...].reshape(1, CH), *parts[1])
+
+    def row_of(s, r):
+        if r == 0:
+            return keep_if(has_up, unpack_row(HA.at[s]))
+        return widen(P2[s, span(r - 1), :].astype(F32))
 
     def dprep(s, L):
         for o in QUAD:
-            xs = [X2[s, span(2 * o + dy), :] for dy in TRI]
+            xs = [row_of(s, 2 * o + dy) for dy in TRI]
             for dy in TRI:
-                L[span(o), span(dy, MAIN)] = xs[dy][:, :MAIN]
-            store_rest(L, o, *(x[:, MAIN:].astype(F32) for x in xs))
+                L[span(o), span(dy, MAIN)] = xs[dy][:, :MAIN].astype(BF)
+            store_rest(L, o, *(x[:, MAIN:] for x in xs))
 
     def depi(s, Y, zero):
         for o in QUAD:
@@ -595,15 +527,23 @@
 
     def dhalf(t, Lc, Ln, Yc, Yp, zero):
         for n in QUAD:
-            dot_chunk(Lc, W.at[1], Yc, slice(0, NP // 2), n)
+            dot_chunk(Lc, W, Yc, slice(0, NP // 2), n)
         dprep(jnp.minimum(t + 1, NS - 1), Ln)
         depi(lax.rem(t + NS - 1, NS), Yp, zero)
 
     dprep(0, L0)
+    weight_finish(bd[...].reshape(1, CH), W, WR, wm_sem, wr_sem)
 
     def dbody(i, carry):
         t = 2 * i
         zero = nil(i)
+        for s in (t, t + 1):
+            pl.when(s + ahead < NS)(functools.partial(fetch, s + ahead))
+            pl.when(s + 1 < NS)(lambda s=s: take(2, s + 1).wait())
+            put(2, s).start()
+            for k in DUO:
+                take(k, s).wait()
+                put(k, s).start()
         dhalf(t, L0, L1, Y0, Y1, zero)
         dhalf(t + 1, L1, L0, Y1, Y0, zero)
         return carry
@@ -647,26 +587,24 @@
         def out(*shape):
             return jax.ShapeDtypeStruct(shape, BF)
 
-        hand, hand0, halo, ab = pl.pallas_call(
+        hand, halo = pl.pallas_call(
             functools.partial(mega, sp),
-            out_shape=(out(2, NS, NP, CP), out(NS, NP, CH), out(SLOTS, NS, PK, MAIN), jax.ShapeDtypeStruct((2, NS, CP), F32)),
-            in_specs=[vms] * 11 + [any_] * 3, out_specs=(any_, any_, any_, vms),
-            scratch_shapes=[big(), big(), big(), big(NP, CH), vm((3, KP, KP), BF), vm((3, 9, CH, ROW), BF), vm((2, CH, temb_w.shape[1]), BF), vm((3 * NS, CP), F32)] + bufs(NP)
+            out_shape=(out(3, NS, NP, CH), out(NS, PK, MAIN)),
+            in_specs=[vms] * 11 + [any_] * 3, out_specs=(any_, any_),
+            scratch_shapes=[big(), big(), big(), big(NP, CH), vm((SLOTS, KP, KP), BF), vm((SLOTS, 9, CH, ROW), BF), vm((2, CH, temb_w.shape[1]), BF), vm((3 * NS, CP), F32)] + bufs(NP)
             + [vm((NS, OFF, LANE), F32), vm((OFF, LANE), F32), vm((SLOTS, NS, 2, LANE), F32), vm((SLOTS, sp - 1, NS, 2, LANE), F32), vm((2, 3, CP), F32), vm((SLOTS, NS, CP), F32), vm((OFF, CP), F32),
-               edge(4), edge(4), big(PK, MAIN), edge(3), edge(3), big(PK, MAIN), vm((2, NS, NS, LANE), BF),
-               dma((3,)), dma((3,)), dma] + [dma((2,))] * 2 + [dma((SLOTS, len(SUMS)))] * SLOTS + [dma((len(SUMS),))]
-            + [dma((SLOTS, len(SUMS)))] * 2 + [dma((len(SUMS),)), dma((SLOTS, len(SUMS))), dma((4,))],
+               edge(SLOTS + 1), edge(SLOTS), edge(SLOTS - 1), edge(SLOTS), vm((2, NS, NS, LANE), BF),
+               dma((SLOTS,)), dma((SLOTS,)), dma] + [dma((2,))] * 2 + [dma((SLOTS + 1, len(SUMS)))] * 7 + [dma],
             compiler_params=params(collective_id=0, has_side_effects=True), name="mega",
         )(q, w_in, b_in, time_emb, temb_b, gn1_scale, gn1_shift, gn2_scale, gn2_shift, conv1_b, conv2_b, temb_w.transpose(0, 2, 1), conv1_w, conv2_w)
         outs = pl.pallas_call(
             tail,
             out_shape=(out(NS, NP, CH),) * 3 + (out(NS, NP // 4, CH),),
-            in_specs=[any_] * 3 + [vms] * 3 + [any_] * 2, out_specs=(any_,) * 4,
-            scratch_shapes=[big(), big(), edge(4), big(NP, CH), big(NP + ROW), vm((2, KP, KP), BF), vm((2, 9, CH, ROW), BF)] + bufs(NP + ROW)
-            + [big(NP, CH), big(NP, CH), big(NP // 4, CH), vm((4, 3, ROW, LANE), F32),
-               dma((2, NS)), dma((SLOTS, NS)), dma((NS,)), dma((2,)), dma((2,)), dma((3, NS)), dma],
+            in_specs=[any_] * 2 + [vms, any_], out_specs=(any_,) * 4,
+            scratch_shapes=[big(NP, CH)] * 3 + [big(PK, MAIN), vm((KP, KP), BF), vm((9, CH, ROW), BF)] + bufs(NP // 2)
+            + [big(NP // 4, CH), vm((4, 3, ROW, LANE), F32), dma((3, NS)), dma, dma, dma, dma((3, NS)), dma],
             compiler_params=params(), name="tail",
-        )(hand, hand0, halo, ab, conv2_b, down_b, conv2_w, down_w)
+        )(hand, halo, down_b, down_w)
         return tuple(o.reshape(NS, n, m, CH) for o, n, m in zip(outs, [ROWS] * len(TRI) + [ROWS // 2], [ROW] * len(TRI) + [ROW // 2]))
 
     band = P("dp", "sp", None, None)

time: 147 us -> 141 us (0.959); the launches traced: 147 us -> 139 us
  Pallas kernels: 142 us -> 134 us
    pallas_call x1, Pallas kernels: 43 us -> 18.8 us  [program(): pl.pallas_call(tail, out_shape=(out(NS, NP, CH),) * 3 + (out(NS, NP // 4,...]
    pallas_call x1, Pallas kernels: 99.3 us -> 115 us  [program(): pl.pallas_call(functools.partial(mega, sp), out_shape=(out(3, NS, NP, CH)...]
where the time goes in v6:
time: 141 us; the launch traced here: 139 us
  Pallas kernels  134 us (95%)
  local copies, waits for them, and re-layouts  2.3 us (2%)
    pallas_call x1, Pallas kernels, program(): pl.pallas_call(functools.partial(mega, sp), out_shape=(out(3, NS, NP, CH)...  115 us
    pallas_call x1, Pallas kernels, program(): pl.pallas_call(tail, out_shape=(out(NS, NP, CH),) * 3 + (out(NS, NP // 4,...  18.8 us

profile of v6, /device:TPU:0, one launch (start us, length us, event | category | flops | bytes accessed | tf_op | source)
XLA Modules:
  0.0 138.6 jit_solution(1702291131466836132)
XLA Ops:
  0.6 1.2 slice_bitcast_fusion.1
  1.9 1.3 pad_maximum_fusion
  3.1 0.1 copy.23
  3.2 0.3 reshape.28
  3.5 0.7 pad.9.q
  4.2 115.5 %mega.1 = (bf16[3,16,512,320]{3,2,1,0:T(8,128)(2,1)}, bf16[16,80,256]{2,1,0:T(8,128)(2,1)}) custom-call(bf16[16,16,512]{2,1,0:T(8,128)(2,1)} %pad.9.q, bf16[3,3,4,320]{3,2,1,0:T(4,128)(2,1)} %wi.1, bf16[320]{0:T(512)(128)(2,1)} %bi.1, bf16[16,1280]{1,0:T(8,128)(2,1)} %temb.1, bf16[2,320]{1,0:T(2,128)(2,1)} %tb.1, bf16[2,320]{1,0:T(2,128)(2,1)} %g1.1, ...), custom_call_target="tpu_custom_call" | custom-call | tf_op jit(solution)/shard_map/mega/pallas_call | solution.py:590
  119.7 18.8 %tail.1 = (bf16[16,512,320]{2,1,0:T(8,128)(2,1)}, bf16[16,512,320]{2,1,0:T(8,128)(2,1)}, bf16[16,512,320]{2,1,0:T(8,128)(2,1)}, bf16[16,128,320]{2,1,0:T(8,128)(2,1)}) custom-call(bf16[3,16,512,320]{3,2,1,0:T(8,128)(2,1)} %get-tuple-element.10.hand, bf16[16,80,256]{2,1,0:T(8,128)(2,1)} %get-tuple-element.11.halo, bf16[320]{0:T(512)(128)(2,1)} %bd.1, ...), custom_call_target="tpu_custom_call" | custom-call | tf_op jit(solution)/shard_map/tail/pallas_call | solution.py:600
